TPU v7x, 32 devices: a whole 2x2x4 slice. The times are simulated.
32 devices in a mesh: srow: 4 (over y, core), scol: 8 (over z, x).
Axes of the slice: x: 2, y: 2, z: 4, core: 2. Of those that a mesh axis runs over, the one named last changes fastest.
Arguments:
- loads: float32 [4, 16, 4, 128], P('srow', 'scol'), may hold values from -6 to 6
- local_inverse: float32 [4, 16, 128, 128], P('srow', 'scol'), as said below
- dirichlet: float32 [4, 16, 128, 128], P('srow', 'scol'), as said below
- corner_coupling: float32 [4, 16, 128], P('srow', 'scol'), may hold values from -4 to 4
- coarse_inverse: float32 [4, 16, 16], P('srow', 'scol'), as said below
- partner: int32 [4, 16, 128], P('srow', 'scol'), may hold values from -1 to 31, as said below
Outputs:
- multipliers: float32 [4, 16, 4, 128], P('srow', 'scol')
- residual: float32 [4, 16, 4, 128], P('srow', 'scol')
Inputs may be any that keep to these rules, and one draw needn't show every extreme that they name: `partner`: on each edge of each subdomain the first n entries, for some n of 1 to 32, are the positions 0 to n - 1 in order or reversed, the rest are -1; the two subdomains sharing an edge have the same n and mutually inverse lists. `local_inverse`: each block is symmetric positive definite. `dirichlet`: each block is symmetric positive definite. `coarse_inverse`: each band's matrix is symmetric positive definite.
All inputs are finite; a program needn't handle non-finite values.
Results may differ from a plain program's by a relative error of at most 0.0003.
Values sent between devices are 32-bit elements; how exact they have to be, the bound alone decides.
A program may use at most 64 MiB of HBM per device.

v0:
```python
import jax
import jax.numpy as jnp
from jax import lax
from jax.sharding import PartitionSpec as P

ITERS = 3


precise = lax.Precision.HIGHEST


def with_halo(cells, sides, width):
    for axis, dim in sides:
        count = lax.axis_size(axis)
        head = lax.slice_in_dim(cells, 0, width, axis=dim)
        tail = lax.slice_in_dim(cells, cells.shape[dim] - width, cells.shape[dim], axis=dim)
        cells = jnp.concatenate(
            [
                lax.ppermute(tail, axis, [(i, (i + 1) % count) for i in range(count)]),
                cells,
                lax.ppermute(head, axis, [((i + 1) % count, i) for i in range(count)]),
            ],
            axis=dim,
        )
    return cells


def facing_edges(values):
    edge_len = values.shape[-1] // 4
    sideways = with_halo(values[..., 0 : 2 * edge_len], (("scol", 1),), 1)
    vertical = with_halo(values[..., 2 * edge_len :], (("srow", 0),), 1)
    west_side = sideways[:, :-2, :, edge_len : 2 * edge_len]
    east_side = sideways[:, 2:, :, 0:edge_len]
    south_side = vertical[:-2, :, :, edge_len : 2 * edge_len]
    north_side = vertical[2:, :, :, 0:edge_len]
    return jnp.concatenate([west_side, east_side, south_side, north_side], axis=-1)


def jump(values, partner):
    edge_len = values.shape[-1] // 4
    facing = facing_edges(values)
    offset = jnp.arange(values.shape[-1], dtype=jnp.int32) // edge_len * edge_len
    position = jnp.clip(partner, 0, edge_len - 1) + offset
    position = jnp.broadcast_to(position[:, :, None, :], values.shape)
    picked = jnp.take_along_axis(facing, position, axis=-1)
    return jnp.where(partner[:, :, None, :] >= 0, values - picked, jnp.zeros_like(values))


def apply_inverse(values, local_inverse, corner_coupling, coarse_inverse):
    sub_rows, sub_cols, rhs_count, width = values.shape
    blocks = jnp.einsum("ijab,ijrb->ijra", local_inverse, values, precision=precise)
    coarse_in = jnp.einsum("ijb,ijrb->ijr", corner_coupling, values, precision=precise)
    coarse_in = coarse_in.reshape(sub_rows * sub_cols, rhs_count)
    band_rows = coarse_inverse[0]
    coarse_out = jnp.dot(
        band_rows,
        lax.all_gather(coarse_in, "scol", axis=0, tiled=True),
        precision=precise,
        preferred_element_type=jnp.float32,
    )
    coarse_out = coarse_out.reshape(sub_rows, sub_cols, rhs_count)
    return blocks + corner_coupling[:, :, None, :] * coarse_out[..., None]


def inner(left, right):
    return jnp.sum(left * right, axis=(0, 1, 3))


def global_sums(first_dot, second_dot):
    return lax.psum((first_dot, second_dot), ("srow", "scol"))


def scaled(coef, values):
    return coef[None, None, :, None] * values


def body(loads, local_inverse, dirichlet, corner_coupling, coarse_inverse, partner):

    def operator(values):
        spread = jump(values, partner)
        return jump(apply_inverse(spread, local_inverse, corner_coupling, coarse_inverse), partner)

    def precond(values):
        spread = jump(values, partner)
        return jump(jnp.einsum("ijab,ijrb->ijra", dirichlet, spread, precision=precise), partner)

    right = operator(loads)
    multipliers = jnp.zeros_like(right)
    residual = right
    precon = precond(residual)
    image = operator(precon)
    gamma, curvature = global_sums(inner(residual, precon), inner(precon, image))
    step_size = gamma / curvature
    search = precon
    along = image
    for iteration in range(ITERS):
        multipliers = multipliers + scaled(step_size, search)
        residual = residual - scaled(step_size, along)
        if iteration + 1 < ITERS:
            precon = precond(residual)
            image = operator(precon)
            gamma_new, curvature = global_sums(inner(residual, precon), inner(precon, image))
            dir_ratio = gamma_new / gamma
            step_size = gamma_new / (curvature - dir_ratio * gamma_new / step_size)
            search = precon + scaled(dir_ratio, search)
            along = image + scaled(dir_ratio, along)
            gamma = gamma_new
    return (multipliers, residual)


def solution(mesh):
    return jax.shard_map(
        body,
        mesh=mesh,
        in_specs=(
            P("srow", "scol", None, None),
            P("srow", "scol", None, None),
            P("srow", "scol", None, None),
            P("srow", "scol", None),
            P("srow", "scol", None),
            P("srow", "scol", None),
        ),
        out_specs=(P("srow", "scol", None, None), P("srow", "scol", None, None)),
        check_vma=False,
    )
```

profile of v0, /device:TPU:0, one launch (start us, length us, event | category | flops | bytes accessed | tf_op | source)
XLA Modules:
  0.0 464.1 jit_solution(16173901481340105120)
XLA Ops:
  2.0 1.9 collective-permute-start.3
  4.0 2.3 collective-permute-start
  6.2 3.1 collective-permute-start.1
  10.9 9.6 %gather_fusion = f32[1024]{0:T(1024)S(1)} fusion(f32[2,4,128]{2,1,0:T(4,128)S(1)} %fusion.69, s32[1024]{0:T(1024)S(1)} %bitcast.196), kind=kCustom, calls=%fused_computation.clone | custom fusion | bytes 20480 | tf_op jit(solution)/shard_map/jit(take_along_axis)/gather | solution.py:45
  21.3 21.1 %all-gather = f32[8,2,4]{2,1,0:T(2,128)S(1)} all-gather(f32[1,2,4]{2,1,0:T(2,128)S(1)} %bitcast.256), channel_id=1, replica_groups=mesh['srow'=4,'scol'=8] {'scol'}, dimensions={0}, use_global_device_ids=true | all-gather | bytes 288 | tf_op jit(solution)/shard_map/all_gather | solution.py:57
  43.6 1.7 collective-permute-start.7
  45.4 4.7 %collective-permute-start.5 = (f32[1,1,4,64]{3,2,1,0:T(4,128)S(1)}, f32[1,1,4,64]{3,2,1,0:T(4,128)S(1)}, u32[]{:S(2)}, u32[]{:S(2)}) collective-permute-start(f32[1,1,4,64]{3,2,1,0:T(4,128)S(1)} %get-tuple-element.76), channel_id=1, source_target_pairs={{1,0},{2,1},{3,2},{4,3},{5,4},{6,5},{7,6},{0,7},{9,8},{10,9},{11,1... | collective-permute-start | bytes 3080 | tf_op jit(solution)/shard_map/ppermute | solution.py:21
  50.2 1.5 collective-permute-done.4
  51.7 9.6 %gather_fusion.1 = f32[1024]{0:T(1024)S(1)} fusion(f32[2,4,128]{2,1,0:T(4,128)S(1)} %fusion.65, s32[1024]{0:T(1024)S(1)} %bitcast.197), kind=kCustom, calls=%fused_computation.1.clone | custom fusion | bytes 20480 | tf_op jit(solution)/shard_map/jit(take_along_axis)/gather | solution.py:45
  61.5 1.7 collective-permute-start.11
  63.2 4.7 %collective-permute-start.9 = (f32[1,1,4,64]{3,2,1,0:T(4,128)S(1)}, f32[1,1,4,64]{3,2,1,0:T(4,128)S(1)}, u32[]{:S(2)}, u32[]{:S(2)}) collective-permute-start(f32[1,1,4,64]{3,2,1,0:T(4,128)S(1)} %get-tuple-element.72), channel_id=1, source_target_pairs={{1,0},{2,1},{3,2},{4,3},{5,4},{6,5},{7,6},{0,7},{9,8},{10,9},{11,1... | collective-permute-start | bytes 3080 | tf_op jit(solution)/shard_map/ppermute | solution.py:21
  68.0 1.5 collective-permute-done.8
  69.6 9.6 %gather_fusion.2 = f32[1024]{0:T(1024)S(1)} fusion(f32[2,4,128]{2,1,0:T(4,128)S(1)} %fusion.61, s32[1024]{0:T(1024)S(1)} %bitcast.198), kind=kCustom, calls=%fused_computation.2.clone | custom fusion | bytes 20480 | tf_op jit(solution)/shard_map/jit(take_along_axis)/gather | solution.py:45
  79.6 1.8 collective-permute-start.15
  81.3 4.7 %collective-permute-start.13 = (f32[1,1,4,64]{3,2,1,0:T(4,128)S(1)}, f32[1,1,4,64]{3,2,1,0:T(4,128)S(1)}, u32[]{:S(2)}, u32[]{:S(2)}) collective-permute-start(f32[1,1,4,64]{3,2,1,0:T(4,128)S(1)} %get-tuple-element.68), channel_id=1, source_target_pairs={{1,0},{2,1},{3,2},{4,3},{5,4},{6,5},{7,6},{0,7},{9,8},{10,9},{11,1... | collective-permute-start | bytes 3080 | tf_op jit(solution)/shard_map/ppermute | solution.py:21
  86.1 1.5 collective-permute-done.12
  87.7 9.6 %gather_fusion.3 = f32[1024]{0:T(1024)S(1)} fusion(f32[2,4,128]{2,1,0:T(4,128)S(1)} %fusion.57, s32[1024]{0:T(1024)S(1)} %bitcast.199), kind=kCustom, calls=%fused_computation.3.clone | custom fusion | bytes 20480 | tf_op jit(solution)/shard_map/jit(take_along_axis)/gather | solution.py:45
  97.4 1.7 collective-permute-start.19
  99.2 4.7 %collective-permute-start.17 = (f32[1,1,4,64]{3,2,1,0:T(4,128)S(1)}, f32[1,1,4,64]{3,2,1,0:T(4,128)S(1)}, u32[]{:S(2)}, u32[]{:S(2)}) collective-permute-start(f32[1,1,4,64]{3,2,1,0:T(4,128)S(1)} %get-tuple-element.64), channel_id=1, source_target_pairs={{1,0},{2,1},{3,2},{4,3},{5,4},{6,5},{7,6},{0,7},{9,8},{10,9},{11,1... | collective-permute-start | bytes 3080 | tf_op jit(solution)/shard_map/ppermute | solution.py:21
  104.0 1.5 collective-permute-done.16
  105.5 9.6 %gather_fusion.4 = f32[1024]{0:T(1024)S(1)} fusion(f32[2,4,128]{2,1,0:T(4,128)S(1)} %fusion.53, s32[1024]{0:T(1024)S(1)} %bitcast.200), kind=kCustom, calls=%fused_computation.4.clone | custom fusion | bytes 20480 | tf_op jit(solution)/shard_map/jit(take_along_axis)/gather | solution.py:45
  115.3 21.0 %all-gather.1 = f32[8,2,4]{2,1,0:T(2,128)S(1)} all-gather(f32[1,2,4]{2,1,0:T(2,128)S(1)} %bitcast.257), channel_id=1, replica_groups=mesh['srow'=4,'scol'=8] {'scol'}, dimensions={0}, use_global_device_ids=true | all-gather | bytes 288 | tf_op jit(solution)/shard_map/all_gather | solution.py:57
  136.8 1.7 collective-permute-start.23
  138.6 4.7 %collective-permute-start.21 = (f32[1,1,4,64]{3,2,1,0:T(4,128)S(1)}, f32[1,1,4,64]{3,2,1,0:T(4,128)S(1)}, u32[]{:S(2)}, u32[]{:S(2)}) collective-permute-start(f32[1,1,4,64]{3,2,1,0:T(4,128)S(1)} %get-tuple-element.60), channel_id=1, source_target_pairs={{1,0},{2,1},{3,2},{4,3},{5,4},{6,5},{7,6},{0,7},{9,8},{10,9},{11,1... | collective-permute-start | bytes 3080 | tf_op jit(solution)/shard_map/ppermute | solution.py:21
  143.4 1.5 collective-permute-done.20
  144.9 9.6 %gather_fusion.5 = f32[1024]{0:T(1024)S(1)} fusion(f32[2,4,128]{2,1,0:T(4,128)S(1)} %fusion.49, s32[1024]{0:T(1024)S(1)} %bitcast.201), kind=kCustom, calls=%fused_computation.5.clone | custom fusion | bytes 20480 | tf_op jit(solution)/shard_map/jit(take_along_axis)/gather | solution.py:45
  154.7 40.2 %all-reduce.2 = (f32[4]{0:T(128)S(1)}, f32[4]{0:T(128)S(1)}) all-reduce(f32[4]{0:T(128)S(1)} %get-tuple-element.8, f32[4]{0:T(128)S(1)} %get-tuple-element.7), channel_id=1, replica_groups=mesh['srow'=4,'scol'=8] {'srow','scol'}, use_global_device_ids=true, to_apply=%region_1.3 | all-reduce | flops 8 | bytes 64 | tf_op jit(solution)/shard_map/psum | solution.py:70
  195.1 1.7 collective-permute-start.27
  196.8 2.3 collective-permute-start.24
  199.1 2.4 collective-permute-start.25
  201.6 1.5 collective-permute-done.24
  203.2 9.6 %gather_fusion.6 = f32[1024]{0:T(1024)S(1)} fusion(f32[2,4,128]{2,1,0:T(4,128)S(1)} %fusion.45, s32[1024]{0:T(1024)S(1)} %bitcast.202), kind=kCustom, calls=%fused_computation.6.clone | custom fusion | bytes 20480 | tf_op jit(solution)/shard_map/jit(take_along_axis)/gather | solution.py:45
  213.2 1.8 collective-permute-start.31
  214.9 1.8 collective-permute-start.28
  216.7 2.9 collective-permute-start.29
  219.7 1.5 collective-permute-done.28
  221.3 9.6 %gather_fusion.7 = f32[1024]{0:T(1024)S(1)} fusion(f32[2,4,128]{2,1,0:T(4,128)S(1)} %fusion.41, s32[1024]{0:T(1024)S(1)} %bitcast.203), kind=kCustom, calls=%fused_computation.7.clone | custom fusion | bytes 20480 | tf_op jit(solution)/shard_map/jit(take_along_axis)/gather | solution.py:45
  231.0 1.7 collective-permute-start.35
  234.1 3.4 collective-permute-start.33
  237.6 1.5 collective-permute-done.32
  239.1 9.6 %gather_fusion.8 = f32[1024]{0:T(1024)S(1)} fusion(f32[2,4,128]{2,1,0:T(4,128)S(1)} %fusion.37, s32[1024]{0:T(1024)S(1)} %bitcast.204), kind=kCustom, calls=%fused_computation.8.clone | custom fusion | bytes 20480 | tf_op jit(solution)/shard_map/jit(take_along_axis)/gather | solution.py:45
  248.9 21.0 %all-gather.2 = f32[8,2,4]{2,1,0:T(2,128)S(1)} all-gather(f32[1,2,4]{2,1,0:T(2,128)S(1)} %bitcast.258), channel_id=1, replica_groups=mesh['srow'=4,'scol'=8] {'scol'}, dimensions={0}, use_global_device_ids=true | all-gather | bytes 288 | tf_op jit(solution)/shard_map/all_gather | solution.py:57
  270.4 1.7 collective-permute-start.39
  272.2 4.7 %collective-permute-start.37 = (f32[1,1,4,64]{3,2,1,0:T(4,128)S(1)}, f32[1,1,4,64]{3,2,1,0:T(4,128)S(1)}, u32[]{:S(2)}, u32[]{:S(2)}) collective-permute-start(f32[1,1,4,64]{3,2,1,0:T(4,128)S(1)} %get-tuple-element.44), channel_id=1, source_target_pairs={{1,0},{2,1},{3,2},{4,3},{5,4},{6,5},{7,6},{0,7},{9,8},{10,9},{11,1... | collective-permute-start | bytes 3080 | tf_op jit(solution)/shard_map/ppermute | solution.py:21
  278.5 9.6 %gather_fusion.9 = f32[1024]{0:T(1024)S(1)} fusion(f32[2,4,128]{2,1,0:T(4,128)S(1)} %fusion.33, s32[1024]{0:T(1024)S(1)} %bitcast.205), kind=kCustom, calls=%fused_computation.9.clone | custom fusion | bytes 20480 | tf_op jit(solution)/shard_map/jit(take_along_axis)/gather | solution.py:45
  288.3 40.8 %all-reduce.1 = (f32[4]{0:T(128)S(1)}, f32[4]{0:T(128)S(1)}) all-reduce(f32[4]{0:T(128)S(1)} %get-tuple-element.6, f32[4]{0:T(128)S(1)} %get-tuple-element.5), channel_id=1, replica_groups=mesh['srow'=4,'scol'=8] {'srow','scol'}, use_global_device_ids=true, to_apply=%region_5.7 | all-reduce | flops 8 | bytes 64 | tf_op jit(solution)/shard_map/psum | solution.py:70
  329.3 1.8 collective-permute-start.43
  331.1 2.3 collective-permute-start.40
  333.3 2.4 collective-permute-start.41
  335.9 1.5 collective-permute-done.40
  337.4 9.6 %gather_fusion.10 = f32[1024]{0:T(1024)S(1)} fusion(f32[2,4,128]{2,1,0:T(4,128)S(1)} %fusion.29, s32[1024]{0:T(1024)S(1)} %bitcast.206), kind=kCustom, calls=%fused_computation.10.clone | custom fusion | bytes 20480 | tf_op jit(solution)/shard_map/jit(take_along_axis)/gather | solution.py:45
  347.4 1.8 collective-permute-start.47
  349.2 1.8 collective-permute-start.44
  351.0 2.9 collective-permute-start.45
  355.5 9.6 %gather_fusion.11 = f32[1024]{0:T(1024)S(1)} fusion(f32[2,4,128]{2,1,0:T(4,128)S(1)} %fusion.25, s32[1024]{0:T(1024)S(1)} %bitcast.207), kind=kCustom, calls=%fused_computation.11.clone | custom fusion | bytes 20480 | tf_op jit(solution)/shard_map/jit(take_along_axis)/gather | solution.py:45
  365.3 1.7 collective-permute-start.51
  368.4 3.4 collective-permute-start.49
  371.8 1.5 collective-permute-done.48
  373.4 9.6 %gather_fusion.12 = f32[1024]{0:T(1024)S(1)} fusion(f32[2,4,128]{2,1,0:T(4,128)S(1)} %fusion.21, s32[1024]{0:T(1024)S(1)} %bitcast.208), kind=kCustom, calls=%fused_computation.12.clone | custom fusion | bytes 20480 | tf_op jit(solution)/shard_map/jit(take_along_axis)/gather | solution.py:45
  383.1 21.0 %all-gather.3 = f32[8,2,4]{2,1,0:T(2,128)S(1)} all-gather(f32[1,2,4]{2,1,0:T(2,128)S(1)} %bitcast.259), channel_id=1, replica_groups=mesh['srow'=4,'scol'=8] {'scol'}, dimensions={0}, use_global_device_ids=true | all-gather | bytes 288 | tf_op jit(solution)/shard_map/all_gather | solution.py:57
  404.7 1.7 collective-permute-start.55
  406.4 4.7 %collective-permute-start.53 = (f32[1,1,4,64]{3,2,1,0:T(4,128)S(1)}, f32[1,1,4,64]{3,2,1,0:T(4,128)S(1)}, u32[]{:S(2)}, u32[]{:S(2)}) collective-permute-start(f32[1,1,4,64]{3,2,1,0:T(4,128)S(1)} %get-tuple-element.28), channel_id=1, source_target_pairs={{1,0},{2,1},{3,2},{4,3},{5,4},{6,5},{7,6},{0,7},{9,8},{10,9},{11,1... | collective-permute-start | bytes 3080 | tf_op jit(solution)/shard_map/ppermute | solution.py:21
  412.8 9.6 %gather_fusion.13 = f32[1024]{0:T(1024)S(1)} fusion(f32[2,4,128]{2,1,0:T(4,128)S(1)} %fusion.17, s32[1024]{0:T(1024)S(1)} %bitcast.209), kind=kCustom, calls=%fused_computation.13.clone | custom fusion | bytes 20480 | tf_op jit(solution)/shard_map/jit(take_along_axis)/gather | solution.py:45
  422.5 40.8 %all-reduce = (f32[4]{0:T(128)S(1)}, f32[4]{0:T(128)S(1)}) all-reduce(f32[4]{0:T(128)S(1)} %get-tuple-element.4, f32[4]{0:T(128)S(1)} %get-tuple-element.3), channel_id=1, replica_groups=mesh['srow'=4,'scol'=8] {'srow','scol'}, use_global_device_ids=true, to_apply=%region_9.11 | all-reduce | flops 8 | bytes 64 | tf_op jit(solution)/shard_map/psum | solution.py:70
  (171 shorter events, 19.1 us)
Async XLA Ops:
  0.6 42.6 %copy-start = (f32[1,2,128,128]{3,2,1,0:T(8,128)S(1)}, f32[1,2,128,128]{3,2,1,0:T(8,128)}, u32[]{:S(2)}) copy-start(f32[1,2,128,128]{3,2,1,0:T(8,128)} %param.9) | copy-start | bytes 393220
  0.6 3.3 copy-start.2
  1.5 7.9 %collective-permute-start.2 = (f32[1,2,4,64]{3,2,1,0:T(4,128)S(1)}, f32[1,2,4,64]{3,2,1,0:T(4,128)S(1)}, u32[]{:S(2)}, u32[]{:S(2)}) collective-permute-start(f32[1,2,4,64]{3,2,1,0:T(4,128)S(1)} %get-tuple-element.77), channel_id=1, source_target_pairs={{0,8},{8,16},{16,24},{24,0},{1,9},{9,17},{17,25},{25,1},{2,10},{10... | collective-permute-start | bytes 6152 | tf_op jit(solution)/shard_map/ppermute | solution.py:19
  2.0 8.8 %collective-permute-start.3 = (f32[1,2,4,64]{3,2,1,0:T(4,128)S(1)}, f32[1,2,4,64]{3,2,1,0:T(4,128)S(1)}, u32[]{:S(2)}, u32[]{:S(2)}) collective-permute-start(f32[1,2,4,64]{3,2,1,0:T(4,128)S(1)} %get-tuple-element.77), channel_id=1, source_target_pairs={{8,0},{16,8},{24,16},{0,24},{9,1},{17,9},{25,17},{1,25},{10,2},{18... | collective-permute-start | bytes 6152 | tf_op jit(solution)/shard_map/ppermute | solution.py:21
  4.0 6.9 %collective-permute-start = (f32[1,1,4,64]{3,2,1,0:T(4,128)S(1)}, f32[1,1,4,64]{3,2,1,0:T(4,128)S(1)}, u32[]{:S(2)}, u32[]{:S(2)}) collective-permute-start(f32[1,1,4,64]{3,2,1,0:T(4,128)S(1)} %get-tuple-element.79), channel_id=1, source_target_pairs={{0,1},{1,2},{2,3},{3,4},{4,5},{5,6},{6,7},{7,0},{8,9},{9,10},{10,1... | collective-permute-start | bytes 3080 | tf_op jit(solution)/shard_map/ppermute | solution.py:19
  6.2 3.1 copy-start.5
  6.2 4.6 collective-permute-start.1
  20.5 0.7 copy-start.3
  42.4 0.7 copy-start.4
  43.6 6.5 %collective-permute-start.6 = (f32[1,2,4,64]{3,2,1,0:T(4,128)S(1)}, f32[1,2,4,64]{3,2,1,0:T(4,128)S(1)}, u32[]{:S(2)}, u32[]{:S(2)}) collective-permute-start(f32[1,2,4,64]{3,2,1,0:T(4,128)S(1)} %get-tuple-element.73), channel_id=1, source_target_pairs={{0,8},{8,16},{16,24},{24,0},{1,9},{9,17},{17,25},{25,1},{2,10},{10... | collective-permute-start | bytes 6152 | tf_op jit(solution)/shard_map/ppermute | solution.py:19
  43.6 8.0 %collective-permute-start.7 = (f32[1,2,4,64]{3,2,1,0:T(4,128)S(1)}, f32[1,2,4,64]{3,2,1,0:T(4,128)S(1)}, u32[]{:S(2)}, u32[]{:S(2)}) collective-permute-start(f32[1,2,4,64]{3,2,1,0:T(4,128)S(1)} %get-tuple-element.73), channel_id=1, source_target_pairs={{8,0},{16,8},{24,16},{0,24},{9,1},{17,9},{25,17},{1,25},{10,2},{18... | collective-permute-start | bytes 6152 | tf_op jit(solution)/shard_map/ppermute | solution.py:21
  45.4 6.3 %collective-permute-start.4 = (f32[1,1,4,64]{3,2,1,0:T(4,128)S(1)}, f32[1,1,4,64]{3,2,1,0:T(4,128)S(1)}, u32[]{:S(2)}, u32[]{:S(2)}) collective-permute-start(f32[1,1,4,64]{3,2,1,0:T(4,128)S(1)} %get-tuple-element.75), channel_id=1, source_target_pairs={{0,1},{1,2},{2,3},{3,4},{4,5},{5,6},{6,7},{7,0},{8,9},{9,10},{10,1... | collective-permute-start | bytes 3080 | tf_op jit(solution)/shard_map/ppermute | solution.py:19
  45.4 6.3 %collective-permute-start.5 = (f32[1,1,4,64]{3,2,1,0:T(4,128)S(1)}, f32[1,1,4,64]{3,2,1,0:T(4,128)S(1)}, u32[]{:S(2)}, u32[]{:S(2)}) collective-permute-start(f32[1,1,4,64]{3,2,1,0:T(4,128)S(1)} %get-tuple-element.76), channel_id=1, source_target_pairs={{1,0},{2,1},{3,2},{4,3},{5,4},{6,5},{7,6},{0,7},{9,8},{10,9},{11,1... | collective-permute-start | bytes 3080 | tf_op jit(solution)/shard_map/ppermute | solution.py:21
  61.4 6.5 %collective-permute-start.10 = (f32[1,2,4,64]{3,2,1,0:T(4,128)S(1)}, f32[1,2,4,64]{3,2,1,0:T(4,128)S(1)}, u32[]{:S(2)}, u32[]{:S(2)}) collective-permute-start(f32[1,2,4,64]{3,2,1,0:T(4,128)S(1)} %get-tuple-element.69), channel_id=1, source_target_pairs={{0,8},{8,16},{16,24},{24,0},{1,9},{9,17},{17,25},{25,1},{2,10},{10... | collective-permute-start | bytes 6152 | tf_op jit(solution)/shard_map/ppermute | solution.py:19
  61.5 8.0 %collective-permute-start.11 = (f32[1,2,4,64]{3,2,1,0:T(4,128)S(1)}, f32[1,2,4,64]{3,2,1,0:T(4,128)S(1)}, u32[]{:S(2)}, u32[]{:S(2)}) collective-permute-start(f32[1,2,4,64]{3,2,1,0:T(4,128)S(1)} %get-tuple-element.69), channel_id=1, source_target_pairs={{8,0},{16,8},{24,16},{0,24},{9,1},{17,9},{25,17},{1,25},{10,2},{18... | collective-permute-start | bytes 6152 | tf_op jit(solution)/shard_map/ppermute | solution.py:21
  63.2 6.3 %collective-permute-start.8 = (f32[1,1,4,64]{3,2,1,0:T(4,128)S(1)}, f32[1,1,4,64]{3,2,1,0:T(4,128)S(1)}, u32[]{:S(2)}, u32[]{:S(2)}) collective-permute-start(f32[1,1,4,64]{3,2,1,0:T(4,128)S(1)} %get-tuple-element.71), channel_id=1, source_target_pairs={{0,1},{1,2},{2,3},{3,4},{4,5},{5,6},{6,7},{7,0},{8,9},{9,10},{10,1... | collective-permute-start | bytes 3080 | tf_op jit(solution)/shard_map/ppermute | solution.py:19
  63.2 6.3 %collective-permute-start.9 = (f32[1,1,4,64]{3,2,1,0:T(4,128)S(1)}, f32[1,1,4,64]{3,2,1,0:T(4,128)S(1)}, u32[]{:S(2)}, u32[]{:S(2)}) collective-permute-start(f32[1,1,4,64]{3,2,1,0:T(4,128)S(1)} %get-tuple-element.72), channel_id=1, source_target_pairs={{1,0},{2,1},{3,2},{4,3},{5,4},{6,5},{7,6},{0,7},{9,8},{10,9},{11,1... | collective-permute-start | bytes 3080 | tf_op jit(solution)/shard_map/ppermute | solution.py:21
  69.6 9.6 %copy-start.1 = (f32[1,2,128,128]{3,2,1,0:T(8,128)S(1)}, f32[1,2,128,128]{3,2,1,0:T(8,128)}, u32[]{:S(2)}) copy-start(f32[1,2,128,128]{3,2,1,0:T(8,128)} %param.10) | copy-start | bytes 393220
  79.6 6.5 %collective-permute-start.14 = (f32[1,2,4,64]{3,2,1,0:T(4,128)S(1)}, f32[1,2,4,64]{3,2,1,0:T(4,128)S(1)}, u32[]{:S(2)}, u32[]{:S(2)}) collective-permute-start(f32[1,2,4,64]{3,2,1,0:T(4,128)S(1)} %get-tuple-element.65), channel_id=1, source_target_pairs={{0,8},{8,16},{16,24},{24,0},{1,9},{9,17},{17,25},{25,1},{2,10},{10... | collective-permute-start | bytes 6152 | tf_op jit(solution)/shard_map/ppermute | solution.py:19
  79.6 8.0 %collective-permute-start.15 = (f32[1,2,4,64]{3,2,1,0:T(4,128)S(1)}, f32[1,2,4,64]{3,2,1,0:T(4,128)S(1)}, u32[]{:S(2)}, u32[]{:S(2)}) collective-permute-start(f32[1,2,4,64]{3,2,1,0:T(4,128)S(1)} %get-tuple-element.65), channel_id=1, source_target_pairs={{8,0},{16,8},{24,16},{0,24},{9,1},{17,9},{25,17},{1,25},{10,2},{18... | collective-permute-start | bytes 6152 | tf_op jit(solution)/shard_map/ppermute | solution.py:21
  81.3 6.3 %collective-permute-start.12 = (f32[1,1,4,64]{3,2,1,0:T(4,128)S(1)}, f32[1,1,4,64]{3,2,1,0:T(4,128)S(1)}, u32[]{:S(2)}, u32[]{:S(2)}) collective-permute-start(f32[1,1,4,64]{3,2,1,0:T(4,128)S(1)} %get-tuple-element.67), channel_id=1, source_target_pairs={{0,1},{1,2},{2,3},{3,4},{4,5},{5,6},{6,7},{7,0},{8,9},{9,10},{10,1... | collective-permute-start | bytes 3080 | tf_op jit(solution)/shard_map/ppermute | solution.py:19
  81.3 6.3 %collective-permute-start.13 = (f32[1,1,4,64]{3,2,1,0:T(4,128)S(1)}, f32[1,1,4,64]{3,2,1,0:T(4,128)S(1)}, u32[]{:S(2)}, u32[]{:S(2)}) collective-permute-start(f32[1,1,4,64]{3,2,1,0:T(4,128)S(1)} %get-tuple-element.68), channel_id=1, source_target_pairs={{1,0},{2,1},{3,2},{4,3},{5,4},{6,5},{7,6},{0,7},{9,8},{10,9},{11,1... | collective-permute-start | bytes 3080 | tf_op jit(solution)/shard_map/ppermute | solution.py:21
  97.4 6.5 %collective-permute-start.18 = (f32[1,2,4,64]{3,2,1,0:T(4,128)S(1)}, f32[1,2,4,64]{3,2,1,0:T(4,128)S(1)}, u32[]{:S(2)}, u32[]{:S(2)}) collective-permute-start(f32[1,2,4,64]{3,2,1,0:T(4,128)S(1)} %get-tuple-element.61), channel_id=1, source_target_pairs={{0,8},{8,16},{16,24},{24,0},{1,9},{9,17},{17,25},{25,1},{2,10},{10... | collective-permute-start | bytes 6152 | tf_op jit(solution)/shard_map/ppermute | solution.py:19
  97.4 8.0 %collective-permute-start.19 = (f32[1,2,4,64]{3,2,1,0:T(4,128)S(1)}, f32[1,2,4,64]{3,2,1,0:T(4,128)S(1)}, u32[]{:S(2)}, u32[]{:S(2)}) collective-permute-start(f32[1,2,4,64]{3,2,1,0:T(4,128)S(1)} %get-tuple-element.61), channel_id=1, source_target_pairs={{8,0},{16,8},{24,16},{0,24},{9,1},{17,9},{25,17},{1,25},{10,2},{18... | collective-permute-start | bytes 6152 | tf_op jit(solution)/shard_map/ppermute | solution.py:21
  99.2 6.3 %collective-permute-start.16 = (f32[1,1,4,64]{3,2,1,0:T(4,128)S(1)}, f32[1,1,4,64]{3,2,1,0:T(4,128)S(1)}, u32[]{:S(2)}, u32[]{:S(2)}) collective-permute-start(f32[1,1,4,64]{3,2,1,0:T(4,128)S(1)} %get-tuple-element.63), channel_id=1, source_target_pairs={{0,1},{1,2},{2,3},{3,4},{4,5},{5,6},{6,7},{7,0},{8,9},{9,10},{10,1... | collective-permute-start | bytes 3080 | tf_op jit(solution)/shard_map/ppermute | solution.py:19
  99.2 6.3 %collective-permute-start.17 = (f32[1,1,4,64]{3,2,1,0:T(4,128)S(1)}, f32[1,1,4,64]{3,2,1,0:T(4,128)S(1)}, u32[]{:S(2)}, u32[]{:S(2)}) collective-permute-start(f32[1,1,4,64]{3,2,1,0:T(4,128)S(1)} %get-tuple-element.64), channel_id=1, source_target_pairs={{1,0},{2,1},{3,2},{4,3},{5,4},{6,5},{7,6},{0,7},{9,8},{10,9},{11,1... | collective-permute-start | bytes 3080 | tf_op jit(solution)/shard_map/ppermute | solution.py:21
  136.8 6.5 %collective-permute-start.22 = (f32[1,2,4,64]{3,2,1,0:T(4,128)S(1)}, f32[1,2,4,64]{3,2,1,0:T(4,128)S(1)}, u32[]{:S(2)}, u32[]{:S(2)}) collective-permute-start(f32[1,2,4,64]{3,2,1,0:T(4,128)S(1)} %get-tuple-element.57), channel_id=1, source_target_pairs={{0,8},{8,16},{16,24},{24,0},{1,9},{9,17},{17,25},{25,1},{2,10},{10... | collective-permute-start | bytes 6152 | tf_op jit(solution)/shard_map/ppermute | solution.py:19
  136.8 8.0 %collective-permute-start.23 = (f32[1,2,4,64]{3,2,1,0:T(4,128)S(1)}, f32[1,2,4,64]{3,2,1,0:T(4,128)S(1)}, u32[]{:S(2)}, u32[]{:S(2)}) collective-permute-start(f32[1,2,4,64]{3,2,1,0:T(4,128)S(1)} %get-tuple-element.57), channel_id=1, source_target_pairs={{8,0},{16,8},{24,16},{0,24},{9,1},{17,9},{25,17},{1,25},{10,2},{18... | collective-permute-start | bytes 6152 | tf_op jit(solution)/shard_map/ppermute | solution.py:21
  138.6 6.3 %collective-permute-start.20 = (f32[1,1,4,64]{3,2,1,0:T(4,128)S(1)}, f32[1,1,4,64]{3,2,1,0:T(4,128)S(1)}, u32[]{:S(2)}, u32[]{:S(2)}) collective-permute-start(f32[1,1,4,64]{3,2,1,0:T(4,128)S(1)} %get-tuple-element.59), channel_id=1, source_target_pairs={{0,1},{1,2},{2,3},{3,4},{4,5},{5,6},{6,7},{7,0},{8,9},{9,10},{10,1... | collective-permute-start | bytes 3080 | tf_op jit(solution)/shard_map/ppermute | solution.py:19
  138.6 6.3 %collective-permute-start.21 = (f32[1,1,4,64]{3,2,1,0:T(4,128)S(1)}, f32[1,1,4,64]{3,2,1,0:T(4,128)S(1)}, u32[]{:S(2)}, u32[]{:S(2)}) collective-permute-start(f32[1,1,4,64]{3,2,1,0:T(4,128)S(1)} %get-tuple-element.60), channel_id=1, source_target_pairs={{1,0},{2,1},{3,2},{4,3},{5,4},{6,5},{7,6},{0,7},{9,8},{10,9},{11,1... | collective-permute-start | bytes 3080 | tf_op jit(solution)/shard_map/ppermute | solution.py:21
  195.1 6.5 %collective-permute-start.26 = (f32[1,2,4,64]{3,2,1,0:T(4,128)S(1)}, f32[1,2,4,64]{3,2,1,0:T(4,128)S(1)}, u32[]{:S(2)}, u32[]{:S(2)}) collective-permute-start(f32[1,2,4,64]{3,2,1,0:T(4,128)S(1)} %get-tuple-element.53), channel_id=1, source_target_pairs={{0,8},{8,16},{16,24},{24,0},{1,9},{9,17},{17,25},{25,1},{2,10},{10... | collective-permute-start | bytes 6152 | tf_op jit(solution)/shard_map/ppermute | solution.py:19
  195.1 8.0 %collective-permute-start.27 = (f32[1,2,4,64]{3,2,1,0:T(4,128)S(1)}, f32[1,2,4,64]{3,2,1,0:T(4,128)S(1)}, u32[]{:S(2)}, u32[]{:S(2)}) collective-permute-start(f32[1,2,4,64]{3,2,1,0:T(4,128)S(1)} %get-tuple-element.53), channel_id=1, source_target_pairs={{8,0},{16,8},{24,16},{0,24},{9,1},{17,9},{25,17},{1,25},{10,2},{18... | collective-permute-start | bytes 6152 | tf_op jit(solution)/shard_map/ppermute | solution.py:21
  196.8 6.3 %collective-permute-start.24 = (f32[1,1,4,64]{3,2,1,0:T(4,128)S(1)}, f32[1,1,4,64]{3,2,1,0:T(4,128)S(1)}, u32[]{:S(2)}, u32[]{:S(2)}) collective-permute-start(f32[1,1,4,64]{3,2,1,0:T(4,128)S(1)} %get-tuple-element.55), channel_id=1, source_target_pairs={{0,1},{1,2},{2,3},{3,4},{4,5},{5,6},{6,7},{7,0},{8,9},{9,10},{10,1... | collective-permute-start | bytes 3080 | tf_op jit(solution)/shard_map/ppermute | solution.py:19
  199.1 4.0 collective-permute-start.25
  213.2 6.5 %collective-permute-start.30 = (f32[1,2,4,64]{3,2,1,0:T(4,128)S(1)}, f32[1,2,4,64]{3,2,1,0:T(4,128)S(1)}, u32[]{:S(2)}, u32[]{:S(2)}) collective-permute-start(f32[1,2,4,64]{3,2,1,0:T(4,128)S(1)} %get-tuple-element.49), channel_id=1, source_target_pairs={{0,8},{8,16},{16,24},{24,0},{1,9},{9,17},{17,25},{25,1},{2,10},{10... | collective-permute-start | bytes 6152 | tf_op jit(solution)/shard_map/ppermute | solution.py:19
  213.2 8.0 %collective-permute-start.31 = (f32[1,2,4,64]{3,2,1,0:T(4,128)S(1)}, f32[1,2,4,64]{3,2,1,0:T(4,128)S(1)}, u32[]{:S(2)}, u32[]{:S(2)}) collective-permute-start(f32[1,2,4,64]{3,2,1,0:T(4,128)S(1)} %get-tuple-element.49), channel_id=1, source_target_pairs={{8,0},{16,8},{24,16},{0,24},{9,1},{17,9},{25,17},{1,25},{10,2},{18... | collective-permute-start | bytes 6152 | tf_op jit(solution)/shard_map/ppermute | solution.py:21
  214.9 6.3 %collective-permute-start.28 = (f32[1,1,4,64]{3,2,1,0:T(4,128)S(1)}, f32[1,1,4,64]{3,2,1,0:T(4,128)S(1)}, u32[]{:S(2)}, u32[]{:S(2)}) collective-permute-start(f32[1,1,4,64]{3,2,1,0:T(4,128)S(1)} %get-tuple-element.51), channel_id=1, source_target_pairs={{0,1},{1,2},{2,3},{3,4},{4,5},{5,6},{6,7},{7,0},{8,9},{9,10},{10,1... | collective-permute-start | bytes 3080 | tf_op jit(solution)/shard_map/ppermute | solution.py:19
  216.7 4.5 collective-permute-start.29
  231.0 6.5 %collective-permute-start.34 = (f32[1,2,4,64]{3,2,1,0:T(4,128)S(1)}, f32[1,2,4,64]{3,2,1,0:T(4,128)S(1)}, u32[]{:S(2)}, u32[]{:S(2)}) collective-permute-start(f32[1,2,4,64]{3,2,1,0:T(4,128)S(1)} %get-tuple-element.45), channel_id=1, source_target_pairs={{0,8},{8,16},{16,24},{24,0},{1,9},{9,17},{17,25},{25,1},{2,10},{10... | collective-permute-start | bytes 6152 | tf_op jit(solution)/shard_map/ppermute | solution.py:19
  231.0 8.0 %collective-permute-start.35 = (f32[1,2,4,64]{3,2,1,0:T(4,128)S(1)}, f32[1,2,4,64]{3,2,1,0:T(4,128)S(1)}, u32[]{:S(2)}, u32[]{:S(2)}) collective-permute-start(f32[1,2,4,64]{3,2,1,0:T(4,128)S(1)} %get-tuple-element.45), channel_id=1, source_target_pairs={{8,0},{16,8},{24,16},{0,24},{9,1},{17,9},{25,17},{1,25},{10,2},{18... | collective-permute-start | bytes 6152 | tf_op jit(solution)/shard_map/ppermute | solution.py:21
  232.8 6.3 %collective-permute-start.32 = (f32[1,1,4,64]{3,2,1,0:T(4,128)S(1)}, f32[1,1,4,64]{3,2,1,0:T(4,128)S(1)}, u32[]{:S(2)}, u32[]{:S(2)}) collective-permute-start(f32[1,1,4,64]{3,2,1,0:T(4,128)S(1)} %get-tuple-element.47), channel_id=1, source_target_pairs={{0,1},{1,2},{2,3},{3,4},{4,5},{5,6},{6,7},{7,0},{8,9},{9,10},{10,1... | collective-permute-start | bytes 3080 | tf_op jit(solution)/shard_map/ppermute | solution.py:19
  234.1 4.9 %collective-permute-start.33 = (f32[1,1,4,64]{3,2,1,0:T(4,128)S(1)}, f32[1,1,4,64]{3,2,1,0:T(4,128)S(1)}, u32[]{:S(2)}, u32[]{:S(2)}) collective-permute-start(f32[1,1,4,64]{3,2,1,0:T(4,128)S(1)} %get-tuple-element.48), channel_id=1, source_target_pairs={{1,0},{2,1},{3,2},{4,3},{5,4},{6,5},{7,6},{0,7},{9,8},{10,9},{11,1... | collective-permute-start | bytes 3080 | tf_op jit(solution)/shard_map/ppermute | solution.py:21
  270.4 6.5 %collective-permute-start.38 = (f32[1,2,4,64]{3,2,1,0:T(4,128)S(1)}, f32[1,2,4,64]{3,2,1,0:T(4,128)S(1)}, u32[]{:S(2)}, u32[]{:S(2)}) collective-permute-start(f32[1,2,4,64]{3,2,1,0:T(4,128)S(1)} %get-tuple-element.41), channel_id=1, source_target_pairs={{0,8},{8,16},{16,24},{24,0},{1,9},{9,17},{17,25},{25,1},{2,10},{10... | collective-permute-start | bytes 6152 | tf_op jit(solution)/shard_map/ppermute | solution.py:19
  270.4 8.0 %collective-permute-start.39 = (f32[1,2,4,64]{3,2,1,0:T(4,128)S(1)}, f32[1,2,4,64]{3,2,1,0:T(4,128)S(1)}, u32[]{:S(2)}, u32[]{:S(2)}) collective-permute-start(f32[1,2,4,64]{3,2,1,0:T(4,128)S(1)} %get-tuple-element.41), channel_id=1, source_target_pairs={{8,0},{16,8},{24,16},{0,24},{9,1},{17,9},{25,17},{1,25},{10,2},{18... | collective-permute-start | bytes 6152 | tf_op jit(solution)/shard_map/ppermute | solution.py:21
  272.2 6.3 %collective-permute-start.36 = (f32[1,1,4,64]{3,2,1,0:T(4,128)S(1)}, f32[1,1,4,64]{3,2,1,0:T(4,128)S(1)}, u32[]{:S(2)}, u32[]{:S(2)}) collective-permute-start(f32[1,1,4,64]{3,2,1,0:T(4,128)S(1)} %get-tuple-element.43), channel_id=1, source_target_pairs={{0,1},{1,2},{2,3},{3,4},{4,5},{5,6},{6,7},{7,0},{8,9},{9,10},{10,1... | collective-permute-start | bytes 3080 | tf_op jit(solution)/shard_map/ppermute | solution.py:19
  272.2 6.3 %collective-permute-start.37 = (f32[1,1,4,64]{3,2,1,0:T(4,128)S(1)}, f32[1,1,4,64]{3,2,1,0:T(4,128)S(1)}, u32[]{:S(2)}, u32[]{:S(2)}) collective-permute-start(f32[1,1,4,64]{3,2,1,0:T(4,128)S(1)} %get-tuple-element.44), channel_id=1, source_target_pairs={{1,0},{2,1},{3,2},{4,3},{5,4},{6,5},{7,6},{0,7},{9,8},{10,9},{11,1... | collective-permute-start | bytes 3080 | tf_op jit(solution)/shard_map/ppermute | solution.py:21
  329.3 6.5 %collective-permute-start.42 = (f32[1,2,4,64]{3,2,1,0:T(4,128)S(1)}, f32[1,2,4,64]{3,2,1,0:T(4,128)S(1)}, u32[]{:S(2)}, u32[]{:S(2)}) collective-permute-start(f32[1,2,4,64]{3,2,1,0:T(4,128)S(1)} %get-tuple-element.37), channel_id=1, source_target_pairs={{0,8},{8,16},{16,24},{24,0},{1,9},{9,17},{17,25},{25,1},{2,10},{10... | collective-permute-start | bytes 6152 | tf_op jit(solution)/shard_map/ppermute | solution.py:19
  329.3 8.0 %collective-permute-start.43 = (f32[1,2,4,64]{3,2,1,0:T(4,128)S(1)}, f32[1,2,4,64]{3,2,1,0:T(4,128)S(1)}, u32[]{:S(2)}, u32[]{:S(2)}) collective-permute-start(f32[1,2,4,64]{3,2,1,0:T(4,128)S(1)} %get-tuple-element.37), channel_id=1, source_target_pairs={{8,0},{16,8},{24,16},{0,24},{9,1},{17,9},{25,17},{1,25},{10,2},{18... | collective-permute-start | bytes 6152 | tf_op jit(solution)/shard_map/ppermute | solution.py:21
  331.1 6.3 %collective-permute-start.40 = (f32[1,1,4,64]{3,2,1,0:T(4,128)S(1)}, f32[1,1,4,64]{3,2,1,0:T(4,128)S(1)}, u32[]{:S(2)}, u32[]{:S(2)}) collective-permute-start(f32[1,1,4,64]{3,2,1,0:T(4,128)S(1)} %get-tuple-element.39), channel_id=1, source_target_pairs={{0,1},{1,2},{2,3},{3,4},{4,5},{5,6},{6,7},{7,0},{8,9},{9,10},{10,1... | collective-permute-start | bytes 3080 | tf_op jit(solution)/shard_map/ppermute | solution.py:19
  333.3 4.0 collective-permute-start.41
  347.4 6.5 %collective-permute-start.46 = (f32[1,2,4,64]{3,2,1,0:T(4,128)S(1)}, f32[1,2,4,64]{3,2,1,0:T(4,128)S(1)}, u32[]{:S(2)}, u32[]{:S(2)}) collective-permute-start(f32[1,2,4,64]{3,2,1,0:T(4,128)S(1)} %get-tuple-element.33), channel_id=1, source_target_pairs={{0,8},{8,16},{16,24},{24,0},{1,9},{9,17},{17,25},{25,1},{2,10},{10... | collective-permute-start | bytes 6152 | tf_op jit(solution)/shard_map/ppermute | solution.py:19
  347.4 8.0 %collective-permute-start.47 = (f32[1,2,4,64]{3,2,1,0:T(4,128)S(1)}, f32[1,2,4,64]{3,2,1,0:T(4,128)S(1)}, u32[]{:S(2)}, u32[]{:S(2)}) collective-permute-start(f32[1,2,4,64]{3,2,1,0:T(4,128)S(1)} %get-tuple-element.33), channel_id=1, source_target_pairs={{8,0},{16,8},{24,16},{0,24},{9,1},{17,9},{25,17},{1,25},{10,2},{18... | collective-permute-start | bytes 6152 | tf_op jit(solution)/shard_map/ppermute | solution.py:21
  349.2 6.3 %collective-permute-start.44 = (f32[1,1,4,64]{3,2,1,0:T(4,128)S(1)}, f32[1,1,4,64]{3,2,1,0:T(4,128)S(1)}, u32[]{:S(2)}, u32[]{:S(2)}) collective-permute-start(f32[1,1,4,64]{3,2,1,0:T(4,128)S(1)} %get-tuple-element.35), channel_id=1, source_target_pairs={{0,1},{1,2},{2,3},{3,4},{4,5},{5,6},{6,7},{7,0},{8,9},{9,10},{10,1... | collective-permute-start | bytes 3080 | tf_op jit(solution)/shard_map/ppermute | solution.py:19
  351.0 4.5 collective-permute-start.45
  365.2 6.5 %collective-permute-start.50 = (f32[1,2,4,64]{3,2,1,0:T(4,128)S(1)}, f32[1,2,4,64]{3,2,1,0:T(4,128)S(1)}, u32[]{:S(2)}, u32[]{:S(2)}) collective-permute-start(f32[1,2,4,64]{3,2,1,0:T(4,128)S(1)} %get-tuple-element.29), channel_id=1, source_target_pairs={{0,8},{8,16},{16,24},{24,0},{1,9},{9,17},{17,25},{25,1},{2,10},{10... | collective-permute-start | bytes 6152 | tf_op jit(solution)/shard_map/ppermute | solution.py:19
  365.3 8.0 %collective-permute-start.51 = (f32[1,2,4,64]{3,2,1,0:T(4,128)S(1)}, f32[1,2,4,64]{3,2,1,0:T(4,128)S(1)}, u32[]{:S(2)}, u32[]{:S(2)}) collective-permute-start(f32[1,2,4,64]{3,2,1,0:T(4,128)S(1)} %get-tuple-element.29), channel_id=1, source_target_pairs={{8,0},{16,8},{24,16},{0,24},{9,1},{17,9},{25,17},{1,25},{10,2},{18... | collective-permute-start | bytes 6152 | tf_op jit(solution)/shard_map/ppermute | solution.py:21
  367.0 6.3 %collective-permute-start.48 = (f32[1,1,4,64]{3,2,1,0:T(4,128)S(1)}, f32[1,1,4,64]{3,2,1,0:T(4,128)S(1)}, u32[]{:S(2)}, u32[]{:S(2)}) collective-permute-start(f32[1,1,4,64]{3,2,1,0:T(4,128)S(1)} %get-tuple-element.31), channel_id=1, source_target_pairs={{0,1},{1,2},{2,3},{3,4},{4,5},{5,6},{6,7},{7,0},{8,9},{9,10},{10,1... | collective-permute-start | bytes 3080 | tf_op jit(solution)/shard_map/ppermute | solution.py:19
  368.4 4.9 %collective-permute-start.49 = (f32[1,1,4,64]{3,2,1,0:T(4,128)S(1)}, f32[1,1,4,64]{3,2,1,0:T(4,128)S(1)}, u32[]{:S(2)}, u32[]{:S(2)}) collective-permute-start(f32[1,1,4,64]{3,2,1,0:T(4,128)S(1)} %get-tuple-element.32), channel_id=1, source_target_pairs={{1,0},{2,1},{3,2},{4,3},{5,4},{6,5},{7,6},{0,7},{9,8},{10,9},{11,1... | collective-permute-start | bytes 3080 | tf_op jit(solution)/shard_map/ppermute | solution.py:21
  404.6 6.5 %collective-permute-start.54 = (f32[1,2,4,64]{3,2,1,0:T(4,128)S(1)}, f32[1,2,4,64]{3,2,1,0:T(4,128)S(1)}, u32[]{:S(2)}, u32[]{:S(2)}) collective-permute-start(f32[1,2,4,64]{3,2,1,0:T(4,128)S(1)} %get-tuple-element.25), channel_id=1, source_target_pairs={{0,8},{8,16},{16,24},{24,0},{1,9},{9,17},{17,25},{25,1},{2,10},{10... | collective-permute-start | bytes 6152 | tf_op jit(solution)/shard_map/ppermute | solution.py:19
  404.7 8.0 %collective-permute-start.55 = (f32[1,2,4,64]{3,2,1,0:T(4,128)S(1)}, f32[1,2,4,64]{3,2,1,0:T(4,128)S(1)}, u32[]{:S(2)}, u32[]{:S(2)}) collective-permute-start(f32[1,2,4,64]{3,2,1,0:T(4,128)S(1)} %get-tuple-element.25), channel_id=1, source_target_pairs={{8,0},{16,8},{24,16},{0,24},{9,1},{17,9},{25,17},{1,25},{10,2},{18... | collective-permute-start | bytes 6152 | tf_op jit(solution)/shard_map/ppermute | solution.py:21
  406.4 6.3 %collective-permute-start.52 = (f32[1,1,4,64]{3,2,1,0:T(4,128)S(1)}, f32[1,1,4,64]{3,2,1,0:T(4,128)S(1)}, u32[]{:S(2)}, u32[]{:S(2)}) collective-permute-start(f32[1,1,4,64]{3,2,1,0:T(4,128)S(1)} %get-tuple-element.27), channel_id=1, source_target_pairs={{0,1},{1,2},{2,3},{3,4},{4,5},{5,6},{6,7},{7,0},{8,9},{9,10},{10,1... | collective-permute-start | bytes 3080 | tf_op jit(solution)/shard_map/ppermute | solution.py:19
  406.4 6.3 %collective-permute-start.53 = (f32[1,1,4,64]{3,2,1,0:T(4,128)S(1)}, f32[1,1,4,64]{3,2,1,0:T(4,128)S(1)}, u32[]{:S(2)}, u32[]{:S(2)}) collective-permute-start(f32[1,1,4,64]{3,2,1,0:T(4,128)S(1)} %get-tuple-element.28), channel_id=1, source_target_pairs={{1,0},{2,1},{3,2},{4,3},{5,4},{6,5},{7,6},{0,7},{9,8},{10,9},{11,1... | collective-permute-start | bytes 3080 | tf_op jit(solution)/shard_map/ppermute | solution.py:21
where the time goes:
time: 465 us; the launch traced here: 464 us
  blocking collectives  206 us (44%)
  local copies, waits for them, and re-layouts  139 us (30%)
  starting transfers between devices  92 us (20%)
  waiting for transfers between devices  20.7 us (4%)
    gather x14, local copies, waits for them, and re-layouts, jump(): picked = jnp.take_along_axis(facing, position, axis=-1)  134 us
    psum x3, blocking collectives, global_sums(): return lax.psum((first_dot, second_dot), ('srow', 'scol'))  122 us
    all_gather x4, blocking collectives, apply_inverse(): lax.all_gather(coarse_in, 'scol', axis=0, tiled=True)  84.1 us
    ppermute x28, starting transfers between devices, with_halo(): lax.ppermute(head, axis, [((i + 1) % count, i) for i in range(count)])  78.3 us
    ppermute x28, waiting for transfers between devices, with_halo(): lax.ppermute(tail, axis, [(i, (i + 1) % count) for i in range(count)])  20.7 us
    ppermute x28, starting transfers between devices, with_halo(): lax.ppermute(tail, axis, [(i, (i + 1) % count) for i in range(count)])  13.7 us
  transfers between devices with their start and end apart: 56, of which 14 were waited for; matrix products, arithmetic and copies ran while one was open for 0% of the time, Pallas kernels for 0%

commit v1 on v0

v1 whole, which is shorter than its diff:
```python
import functools

import jax
import jax.numpy as jnp
from jax import lax
from jax.experimental import pallas as pl
from jax.experimental.pallas import tpu as pltpu
from jax.sharding import PartitionSpec as P

ITERS = 3
MESH = pl.DeviceIdType.MESH
precise = lax.Precision.HIGHEST
NEAR = ((0, 0), (0, 1), (0, -1), (1, 0), (-1, 0))
FAR = ((1, 1), (1, -1), (-1, 1), (-1, -1), (2, 0), (-2, 0))
UNROLL = 64


def slot_list(nr, nc):
    near, slots = [], []
    for offsets, out in ((NEAR, near), (FAR, None)):
        for di, dj in offsets:
            off = (di % nr, dj % nc)
            if off not in slots:
                slots.append(off)
                if out is not None:
                    out.append(off)
    return near, slots


def kernel(nr, nc, near, slots, sc, nrhs, loads, cpl, cinv, part, linv, dirich, m_out, r_out,
           lbuf, dbuf, loads_n, part_n, cpl_n, kt, ub, qb,
           local_sem, k_send, k_recv, c_send, c_recv, l_send, l_recv, p_send, p_recv, d_send, d_recv,
           u_send, u_recv, q_send, q_recv):
    rows, width = loads.shape
    edge = width // 4
    ndev = nr * nc
    ncols = nc * sc
    lanes = kt.shape[-1]
    i, j = lax.axis_index("srow"), lax.axis_index("scol")

    def target(di, dj):
        return (lax.rem(i - di + nr, nr), lax.rem(j - dj + nc, nc))

    def others(step):
        if ndev <= UNROLL:
            for k in range(1, ndev):
                step(k, k // nc, k % nc)
        else:
            @pl.loop(1, ndev)
            def _(k):
                step(k, lax.div(k, nc), lax.rem(k, nc))

    fetch_l = pltpu.make_async_copy(linv, lbuf, local_sem.at[0])
    fetch_d = pltpu.make_async_copy(dirich, dbuf.at[0], local_sem.at[1])
    fetch_l.start()
    fetch_d.start()

    barrier = pltpu.get_barrier_semaphore()

    def greet(k, di, dj):
        pl.semaphore_signal(barrier, inc=1, device_id=target(di, dj), device_id_type=MESH)

    others(greet)

    row = lax.broadcasted_iota(jnp.int32, (rows, width), 0)
    lane = lax.broadcasted_iota(jnp.int32, (rows, width), 1)
    wrow = lax.broadcasted_iota(jnp.int32, (rows, lanes), 0)
    wlane = lax.broadcasted_iota(jnp.int32, (rows, lanes), 1)
    wrhs = lax.rem(wrow, nrhs)
    wsub = lax.div(wrow, nrhs)
    of_rhs = lax.div(wlane, ncols) == wrhs
    gamma_lane = wlane == nrhs * ncols + wrhs
    curve_lane = wlane == nrhs * ncols + nrhs + wrhs

    def spread(block):
        out = jnp.broadcast_to(block[0:1], (rows, block.shape[1]))
        which = lax.div(lax.broadcasted_iota(jnp.int32, out.shape, 0), nrhs)
        for s in range(1, sc):
            out = jnp.where(which == s, jnp.broadcast_to(block[s : s + 1], out.shape), out)
        return out

    def place(dj):
        column = lax.rem(j + dj, nc) * sc
        return wlane == wrhs * ncols + column + wsub

    tile_lane = lax.broadcasted_iota(jnp.int32, (ncols, lanes), 1)
    tile_row = lax.broadcasted_iota(jnp.int32, (ncols, lanes), 0)
    tiler = jnp.where(lax.rem(tile_lane, ncols) == tile_row, 1.0, 0.0)
    tiled = jnp.dot(spread(cinv[...]), tiler, precision=precise, preferred_element_type=jnp.float32)
    kt[0] = jnp.where(of_rhs, tiled, 0.0)

    pl.semaphore_wait(barrier, ndev - 1)

    def remote(src, dst, send, recv, off):
        copy = pltpu.make_async_remote_copy(
            src_ref=src, dst_ref=dst, send_sem=send, recv_sem=recv,
            device_id=target(*off), device_id_type=MESH)
        copy.start()
        return copy

    load_copies = [remote(loads, loads_n.at[n], l_send.at[n], l_recv.at[n], near[n]) for n in range(1, len(near))]
    part_copies = [remote(part, part_n.at[n], p_send.at[n], p_recv.at[n], near[n]) for n in range(1, len(near))]
    cpl_copies = [remote(cpl, cpl_n.at[n], c_send.at[n], c_recv.at[n], slots[n]) for n in range(1, len(slots))]
    east_off, west_off = (0, 1 % nc), (0, nc - 1)
    d_copies = []
    for n in range(1, len(near)):
        if near[n] == east_off:
            src, dst = dirich.at[pl.ds(0, 1)], dbuf.at[n, pl.ds(0, 1)]
        elif near[n] == west_off:
            src, dst = dirich.at[pl.ds(sc - 1, 1)], dbuf.at[n, pl.ds(sc - 1, 1)]
        else:
            src, dst = dirich, dbuf.at[n]
        d_copies.append((src, dst, d_send.at[n], d_recv.at[n], near[n]))

    def send_k(k, di, dj):
        remote(kt.at[0], kt.at[k], k_send, k_recv, (di, dj))

    others(send_k)
    d_copies = [remote(*args) for args in d_copies]

    def index_of(block):
        partner = spread(block)
        position = jnp.clip(partner, 0, edge - 1) + (edge * (1 - 2 * lax.rem(lax.div(lane, edge), 2)) + lax.div(lane, edge) * edge)
        return position, partner >= 0

    def jump(mine, west_tile, east_tile, south, north, lookup):
        position, active = lookup
        west = jnp.where(row < nrhs, pltpu.roll(west_tile, nrhs, 0), pltpu.roll(mine, nrhs, 0))
        east = jnp.where(row >= rows - nrhs, pltpu.roll(east_tile, rows - nrhs, 0), pltpu.roll(mine, rows - nrhs, 0))
        side = lax.div(lane, edge)
        comb = jnp.where(side == 0, east, jnp.where(side == 1, west, jnp.where(side == 2, north, south)))
        facing = jnp.take_along_axis(comb, position, axis=1, mode="promise_in_bounds")
        return jnp.where(active, mine - facing, 0.0)

    def slot_of(di, dj):
        off = (di % nr, dj % nc)
        return slots.index(off) if off in slots else None

    def jump_at(tiles, di, dj, lookup):
        def tile(a, b):
            n = slot_of(a, b)
            return tiles[n] if n is not None and n in tiles else tiles[slot_of(di, dj)]
        return jump(tiles[slot_of(di, dj)], tile(di, dj - 1), tile(di, dj + 1), tile(di - 1, dj), tile(di + 1, dj), lookup)

    def multiply(values, blocks):
        out = None
        for s, block in blocks:
            term = jnp.dot(values, block, precision=precise, preferred_element_type=jnp.float32)
            out = term if out is None else jnp.where(lax.div(row, nrhs) == s, term, out)
        return out

    def lane_sum(values):
        return jnp.sum(values, axis=1, keepdims=True)

    coupling = spread(cpl[...])
    own_place = place(0)

    def publish(rd, values, dots, wide):
        u = multiply(values, [(s, lbuf[s]) for s in range(sc)])
        ub[rd, 0] = u
        count = len(slots) if wide else len(near)
        for n in range(1, count):
            remote(ub.at[rd, 0], ub.at[rd, n], u_send.at[rd], u_recv.at[rd], slots[n])
        message = jnp.where(own_place, lane_sum(coupling * values), 0.0)
        if dots is not None:
            gamma, factor = dots
            message = jnp.where(gamma_lane, lane_sum(gamma), message)
            message = jnp.where(curve_lane, lane_sum(factor * u), message)
        qb[rd, 0] = jnp.sum(message, axis=0, keepdims=True)

        def send_q(k, di, dj):
            remote(qb.at[rd, 0], qb.at[rd, k], q_send.at[rd], q_recv.at[rd], (di, dj))

        others(send_q)
        return count

    def collect(rd, count, want_dots):
        bytes_q = qb.at[rd, pl.ds(1, ndev - 1)]
        pltpu.make_async_copy(bytes_q, bytes_q, q_recv.at[rd]).wait()
        band = [jnp.broadcast_to(jnp.sum(qb[rd, pl.ds(d * nc, nc)], axis=0), (rows, lanes)) for d in range(nr)]
        cols = {}

        def column(k, d):
            return lane_sum(band[d] * kt[k])

        gamma = curve = None
        if want_dots:
            cross = jnp.zeros((rows, lanes), jnp.float32)
            for d in range(nr):
                total = jnp.zeros((rows, lanes), jnp.float32)
                if ndev <= UNROLL:
                    for e in range(nc):
                        cols[(d, e)] = column(d * nc + e, d)
                        total = total + jnp.where(place(e), cols[(d, e)], 0.0)
                else:
                    def add(e, total):
                        return total + jnp.where(place(e), column(d * nc + e, d), 0.0)
                    total = lax.fori_loop(0, nc, add, total)
                cross = cross + total * band[d]
            everything = functools.reduce(jnp.add, band)
            crossed = jnp.broadcast_to(jnp.sum(cross, axis=0, keepdims=True), (rows, lanes))
            curve = lane_sum(jnp.where(of_rhs, crossed, 0.0) + jnp.where(curve_lane, everything, 0.0))
            gamma = lane_sum(jnp.where(gamma_lane, everything, 0.0))
        bytes_u = ub.at[rd, pl.ds(1, count - 1)]
        pltpu.make_async_copy(bytes_u, bytes_u, u_recv.at[rd]).wait()
        tiles = {}
        for n in range(count):
            off = slots[n]
            if off not in cols:
                cols[off] = column(off[0] * nc + off[1], off[0])
            tiles[n] = ub[rd, n] + couplings[n] * cols[off]
        return tiles, gamma, curve

    for n, copy in enumerate(load_copies):
        copy.wait_recv()
    own_lookup = index_of(part[...])
    load_tiles = {n: (loads[...] if n == 0 else loads_n[n]) for n in range(len(near))}
    start = jump_at(load_tiles, 0, 0, own_lookup)
    fetch_l.wait()
    count = publish(0, start, None, True)

    for copy in part_copies:
        copy.wait_recv()
    for copy in cpl_copies:
        copy.wait_recv()
    lookups = [own_lookup] + [index_of(part_n[n]) for n in range(1, len(near))]
    couplings = [coupling] + [spread(cpl_n[n]) for n in range(1, len(slots))]
    bytes_k = kt.at[pl.ds(1, ndev - 1)]
    pltpu.make_async_copy(bytes_k, bytes_k, k_recv).wait()
    tiles, _, _ = collect(0, count, False)
    residual = [jump_at(tiles, *near[n], lookups[n]) for n in range(len(near))]
    fetch_d.wait()
    for copy in d_copies:
        copy.wait_recv()

    multipliers = jnp.zeros((rows, width), jnp.float32)
    search = along = gamma = step_size = None
    for iteration in range(ITERS):
        rd = iteration + 1
        last = rd == ITERS
        weighted = {}
        for n in range(len(near)):
            if near[n] == east_off:
                blocks = [(0, dbuf[n, 0])]
            elif near[n] == west_off:
                blocks = [(sc - 1, dbuf[n, sc - 1])]
            else:
                blocks = [(s, dbuf[n, s]) for s in range(sc)]
            weighted[n] = multiply(2.0 * residual[n], blocks)
        precon = jump_at(weighted, 0, 0, own_lookup)
        doubled = 2.0 * precon
        count = publish(rd, doubled, (residual[0] * precon, doubled), not last)
        tiles, gamma_new, curve = collect(rd, count, True)
        kept = 1 if last else len(near)
        image = [jump_at(tiles, *near[n], lookups[n]) for n in range(kept)]
        if iteration == 0:
            step_size = gamma_new / curve
            search, along = precon, image
        else:
            ratio = gamma_new / gamma
            step_size = gamma_new / (curve - ratio * gamma_new / step_size)
            search = precon + ratio * search
            along = [image[n] + ratio * along[n] for n in range(kept)]
        gamma = gamma_new
        multipliers = multipliers + step_size * search
        residual = [residual[n] - step_size * along[n] for n in range(kept)]
    m_out[...] = multipliers
    r_out[...] = residual[0]

    for copy in load_copies + part_copies + cpl_copies + d_copies:
        copy.wait_send()
    pltpu.make_async_copy(bytes_k, bytes_k, k_send).wait()
    for rd in range(ITERS + 1):
        bytes_q = qb.at[rd, pl.ds(1, ndev - 1)]
        pltpu.make_async_copy(bytes_q, bytes_q, q_send.at[rd]).wait()
        sent = (len(near) if rd == ITERS else len(slots)) - 1
        bytes_u = ub.at[rd, pl.ds(1, sent)]
        pltpu.make_async_copy(bytes_u, bytes_u, u_send.at[rd]).wait()


def solution(mesh):
    nr, nc = mesh.shape["srow"], mesh.shape["scol"]
    near, slots = slot_list(nr, nc)

    def body(loads, local_inverse, dirichlet, corner_coupling, coarse_inverse, partner):
        sr, sc, nrhs, width = loads.shape
        rows = sr * sc * nrhs
        ndev = nr * nc
        lanes = -(-(nrhs * nc * sc + 2 * nrhs) // 128) * 128
        dma = pltpu.SemaphoreType.DMA
        f32 = jnp.float32
        vmem = pl.BlockSpec(memory_space=pltpu.VMEM)
        hbm = pl.BlockSpec(memory_space=pl.ANY)
        tile = jax.ShapeDtypeStruct((rows, width), f32)
        rounds = ITERS + 1
        m, r = pl.pallas_call(
            functools.partial(kernel, nr, nc, near, slots, sc, nrhs),
            out_shape=(tile, tile),
            in_specs=[vmem, vmem, vmem, vmem, hbm, hbm],
            out_specs=(vmem, vmem),
            scratch_shapes=[
                pltpu.VMEM((sc, width, width), f32),
                pltpu.VMEM((len(near), sc, width, width), f32),
                pltpu.VMEM((len(near), rows, width), f32),
                pltpu.VMEM((len(near), sc, width), jnp.int32),
                pltpu.VMEM((len(slots), sc, width), f32),
                pltpu.VMEM((ndev, rows, lanes), f32),
                pltpu.VMEM((rounds, len(slots), rows, width), f32),
                pltpu.VMEM((rounds, ndev, 1, lanes), f32),
                dma((2,)), dma, dma,
                dma((len(slots),)), dma((len(slots),)),
                dma((len(near),)), dma((len(near),)),
                dma((len(near),)), dma((len(near),)),
                dma((len(near),)), dma((len(near),)),
                dma((rounds,)), dma((rounds,)),
                dma((rounds,)), dma((rounds,)),
            ],
            compiler_params=pltpu.CompilerParams(collective_id=0, has_side_effects=True),
        )(
            loads.reshape(rows, width),
            corner_coupling.reshape(sc, width),
            coarse_inverse.reshape(sc, coarse_inverse.shape[-1]),
            partner.reshape(sc, width),
            local_inverse.reshape(sc, width, width),
            dirichlet.reshape(sc, width, width),
        )
        return m.reshape(loads.shape), r.reshape(loads.shape)

    return jax.shard_map(
        body,
        mesh=mesh,
        in_specs=(
            P("srow", "scol", None, None),
            P("srow", "scol", None, None),
            P("srow", "scol", None, None),
            P("srow", "scol", None),
            P("srow", "scol", None),
            P("srow", "scol", None),
        ),
        out_specs=(P("srow", "scol", None, None), P("srow", "scol", None, None)),
        check_vma=False,
    )
```

time: 465 us -> 36.8 us (0.08)
  blocking collectives: 206 us -> 0 us
  local copies, waits for them, and re-layouts: 139 us -> 1.94 us
  starting transfers between devices: 92 us -> 0 us
  Pallas kernels: 0 us -> 34 us
  waiting for transfers between devices: 20.7 us -> 0 us
    gather x14 -> x0, local copies, waits for them, and re-layouts: 134 us -> none  [jump(): picked = jnp.take_along_axis(facing, position, axis=-1)]
    psum x3 -> x0, blocking collectives: 122 us -> none  [global_sums(): return lax.psum((first_dot, second_dot), ('srow', 'scol'))]
    ppermute x56 -> x0, starting transfers between devices: 92 us -> none  [the longest x28 78.3 us: with_halo(): lax.ppermute(head, axis, [((i + 1) % count, i) for i in range(count)])]
    all_gather x4 -> x0, blocking collectives: 84.1 us -> none  [apply_inverse(): lax.all_gather(coarse_in, 'scol', axis=0, tiled=True)]
    pallas_call x0 -> x1, Pallas kernels: none -> 34 us  [body(): pl.pallas_call(functools.partial(kernel, nr, nc, near, slots, sc, nrhs),...]
    ppermute x56 -> x0, waiting for transfers between devices: 20.7 us -> none  [the longest x28 20.7 us: with_halo(): lax.ppermute(tail, axis, [(i, (i + 1) % count) for i in range(count)])]
  transfers between devices with their start and end apart: 56 -> 0, of which waited for: 14 -> 0; matrix products, arithmetic and copies ran while one was open for 0% -> 0% of each run, Pallas kernels for 0% -> 0%
where the time goes in v1:
time: 36.8 us; the launch traced here: 36.6 us
  Pallas kernels  34 us (92%)
  local copies, waits for them, and re-layouts  1.94 us (5%)
  between operations  0.65 us (2%)
    pallas_call x1, Pallas kernels, body(): pl.pallas_call(functools.partial(kernel, nr, nc, near, slots, sc, nrhs),...  34 us
    unnamed x6, local copies, waits for them, and re-layouts  1.94 us

profile of v1, /device:TPU:0, one launch (start us, length us, event | category | flops | bytes accessed | tf_op | source)
XLA Modules:
  0.0 36.6 jit_solution(1798382821705380268)
XLA Ops:
  0.6 34.0 %shard_map.77 = (f32[8,128]{1,0:T(8,128)}, f32[8,128]{1,0:T(8,128)}) custom-call(f32[8,128]{1,0:T(8,128)} %bitcast.10, f32[2,128]{1,0:T(2,128)} %bitcast.13, f32[2,16]{1,0:T(2,128)} %bitcast.14, s32[2,128]{1,0:T(2,128)} %bitcast.15, f32[2,128,128]{2,1,0:T(8,128)} %bitcast.8, f32[2,128,128]{2,1,0:T(8,128)} %bitcast.9), custom_call_target="tpu_custom_call" | custom-call | tf_op jit(solution)/shard_map/pallas_call | solution.py:296
  34.6 0.0 copy-start.1
  34.7 0.7 %copy-done.1 = f32[8,128]{1,0:T(8,128)S(1)} copy-done((f32[8,128]{1,0:T(8,128)S(1)}, f32[8,128]{1,0:T(8,128)}, u32[]{:S(2)}) %copy-start.1) | copy-done | bytes 4120
  35.3 0.0 copy-start
  35.3 0.6 %copy.10 = f32[1,2,4,128]{3,2,1,0:T(4,128)} copy(f32[1,2,4,128]{3,2,1,0:T(4,128)S(1)} %bitcast.12) | data formatting | bytes 8192
  35.9 0.1 copy-done
  36.0 0.6 %copy.11 = f32[1,2,4,128]{3,2,1,0:T(4,128)} copy(f32[1,2,4,128]{3,2,1,0:T(4,128)S(1)} %bitcast.11) | data formatting | bytes 8192
Async XLA Ops:
  34.6 0.7 %copy-start.1 = (f32[8,128]{1,0:T(8,128)S(1)}, f32[8,128]{1,0:T(8,128)}, u32[]{:S(2)}) copy-start(f32[8,128]{1,0:T(8,128)} %get-tuple-element.4) | copy-start | bytes 12292
  35.3 0.7 %copy-start = (f32[8,128]{1,0:T(8,128)S(1)}, f32[8,128]{1,0:T(8,128)}, u32[]{:S(2)}) copy-start(f32[8,128]{1,0:T(8,128)} %get-tuple-element.5) | copy-start | bytes 12292

commit v2 on v1

--- a/solution.py
+++ b/solution.py
@@ -27,8 +27,8 @@
     return near, slots
 
 
-def kernel(nr, nc, near, slots, sc, nrhs, loads, cpl, cinv, part, linv, dirich, m_out, r_out,
-           lbuf, dbuf, loads_n, part_n, cpl_n, kt, ub, qb,
+def kernel(nr, nc, near, slots, sc, nrhs, loads_in, cpl_in, cinv_in, part_in, linv, dirich, out,
+           loads, cpl, cinv, part, lbuf, dbuf, lpair, dpair, loads_n, part_n, cpl_n, kt, ub, qb,
            local_sem, k_send, k_recv, c_send, c_recv, l_send, l_recv, p_send, p_recv, d_send, d_recv,
            u_send, u_recv, q_send, q_recv):
     rows, width = loads.shape
@@ -50,17 +50,22 @@
             def _(k):
                 step(k, lax.div(k, nc), lax.rem(k, nc))
 
-    fetch_l = pltpu.make_async_copy(linv, lbuf, local_sem.at[0])
-    fetch_d = pltpu.make_async_copy(dirich, dbuf.at[0], local_sem.at[1])
-    fetch_l.start()
-    fetch_d.start()
-
     barrier = pltpu.get_barrier_semaphore()
 
     def greet(k, di, dj):
         pl.semaphore_signal(barrier, inc=1, device_id=target(di, dj), device_id_type=MESH)
 
     others(greet)
+
+    fetches = [
+        pltpu.make_async_copy(src, dst, local_sem.at[n])
+        for n, (src, dst) in enumerate((
+            (cinv_in, cinv), (loads_in, loads), (cpl_in, cpl), (part_in, part),
+            (linv, lbuf), (dirich, dbuf.at[0]),
+        ))
+    ]
+    for fetch in fetches:
+        fetch.start()
 
     row = lax.broadcasted_iota(jnp.int32, (rows, width), 0)
     lane = lax.broadcasted_iota(jnp.int32, (rows, width), 1)
@@ -83,11 +88,34 @@
         column = lax.rem(j + dj, nc) * sc
         return wlane == wrhs * ncols + column + wsub
 
+    def index_of(block):
+        partner = spread(block)
+        position = jnp.clip(partner, 0, edge - 1) + (edge * (1 - 2 * lax.rem(lax.div(lane, edge), 2)) + lax.div(lane, edge) * edge)
+        return position, partner >= 0
+
+    def split(values):
+        high = values.astype(jnp.bfloat16)
+        return high, (values - high.astype(jnp.float32)).astype(jnp.bfloat16)
+
+    def split_into(pair, blocks):
+        for s, block in enumerate(blocks):
+            high, low = split(block)
+            pair[s * width : (s + 1) * width, 0:width] = high
+            pair[s * width : (s + 1) * width, width : 2 * width] = low
+
     tile_lane = lax.broadcasted_iota(jnp.int32, (ncols, lanes), 1)
     tile_row = lax.broadcasted_iota(jnp.int32, (ncols, lanes), 0)
     tiler = jnp.where(lax.rem(tile_lane, ncols) == tile_row, 1.0, 0.0)
+    for fetch in fetches[:4]:
+        fetch.wait()
     tiled = jnp.dot(spread(cinv[...]), tiler, precision=precise, preferred_element_type=jnp.float32)
     kt[0] = jnp.where(of_rhs, tiled, 0.0)
+
+    own_position, own_active = index_of(part[...])
+    coupling = spread(cpl[...])
+    own_place = place(0)
+    fetches[4].wait()
+    split_into(lpair, [lbuf[s] for s in range(sc)])
 
     pl.semaphore_wait(barrier, ndev - 1)
 
@@ -118,11 +146,6 @@
     others(send_k)
     d_copies = [remote(*args) for args in d_copies]
 
-    def index_of(block):
-        partner = spread(block)
-        position = jnp.clip(partner, 0, edge - 1) + (edge * (1 - 2 * lax.rem(lax.div(lane, edge), 2)) + lax.div(lane, edge) * edge)
-        return position, partner >= 0
-
     def jump(mine, west_tile, east_tile, south, north, lookup):
         position, active = lookup
         west = jnp.where(row < nrhs, pltpu.roll(west_tile, nrhs, 0), pltpu.roll(mine, nrhs, 0))
@@ -142,21 +165,20 @@
             return tiles[n] if n is not None and n in tiles else tiles[slot_of(di, dj)]
         return jump(tiles[slot_of(di, dj)], tile(di, dj - 1), tile(di, dj + 1), tile(di - 1, dj), tile(di + 1, dj), lookup)
 
-    def multiply(values, blocks):
-        out = None
-        for s, block in blocks:
-            term = jnp.dot(values, block, precision=precise, preferred_element_type=jnp.float32)
-            out = term if out is None else jnp.where(lax.div(row, nrhs) == s, term, out)
-        return out
+    def multiply(values, pair, count):
+        high, low = split(values)
+        stacked = jnp.concatenate([high.astype(jnp.float32), low.astype(jnp.float32)], axis=0)
+        sub = lax.rem(lax.div(lax.broadcasted_iota(jnp.int32, stacked.shape, 0), nrhs), sc)
+        wide = jnp.concatenate(
+            [jnp.where(sub == (s if s < count - 1 else sc - 1), stacked, 0.0) for s in range(count)], axis=1)
+        product = jnp.dot(wide.astype(jnp.bfloat16), pair, preferred_element_type=jnp.float32)
+        return (product[0:rows, 0:width] + product[rows:, 0:width]) + (product[0:rows, width:] + product[rows:, width:])
 
     def lane_sum(values):
         return jnp.sum(values, axis=1, keepdims=True)
 
-    coupling = spread(cpl[...])
-    own_place = place(0)
-
     def publish(rd, values, dots, wide):
-        u = multiply(values, [(s, lbuf[s]) for s in range(sc)])
+        u = multiply(values, lpair[...], sc)
         ub[rd, 0] = u
         count = len(slots) if wide else len(near)
         for n in range(1, count):
@@ -213,10 +235,9 @@
 
     for n, copy in enumerate(load_copies):
         copy.wait_recv()
-    own_lookup = index_of(part[...])
+    own_lookup = (own_position, own_active)
     load_tiles = {n: (loads[...] if n == 0 else loads_n[n]) for n in range(len(near))}
     start = jump_at(load_tiles, 0, 0, own_lookup)
-    fetch_l.wait()
     count = publish(0, start, None, True)
 
     for copy in part_copies:
@@ -227,11 +248,16 @@
     couplings = [coupling] + [spread(cpl_n[n]) for n in range(1, len(slots))]
     bytes_k = kt.at[pl.ds(1, ndev - 1)]
     pltpu.make_async_copy(bytes_k, bytes_k, k_recv).wait()
+    fetches[5].wait()
+    for copy in d_copies:
+        copy.wait_recv()
+    east, west = near.index(east_off), near.index(west_off)
+    upright = [n for n in range(len(near)) if n not in (east, west)]
+    for n in upright:
+        split_into(dpair.at[n], [dbuf[n, s] for s in range(sc)])
+    split_into(dpair.at[east], [dbuf[east, 0], dbuf[west, sc - 1]])
     tiles, _, _ = collect(0, count, False)
     residual = [jump_at(tiles, *near[n], lookups[n]) for n in range(len(near))]
-    fetch_d.wait()
-    for copy in d_copies:
-        copy.wait_recv()
 
     multipliers = jnp.zeros((rows, width), jnp.float32)
     search = along = gamma = step_size = None
@@ -239,14 +265,10 @@
         rd = iteration + 1
         last = rd == ITERS
         weighted = {}
-        for n in range(len(near)):
-            if near[n] == east_off:
-                blocks = [(0, dbuf[n, 0])]
-            elif near[n] == west_off:
-                blocks = [(sc - 1, dbuf[n, sc - 1])]
-            else:
-                blocks = [(s, dbuf[n, s]) for s in range(sc)]
-            weighted[n] = multiply(2.0 * residual[n], blocks)
+        for n in upright:
+            weighted[n] = multiply(2.0 * residual[n], dpair[n], sc)
+        beside = jnp.where(row < nrhs, residual[east], residual[west])
+        weighted[east] = weighted[west] = multiply(2.0 * beside, dpair[east, pl.ds(0, 2 * width)], 2)
         precon = jump_at(weighted, 0, 0, own_lookup)
         doubled = 2.0 * precon
         count = publish(rd, doubled, (residual[0] * precon, doubled), not last)
@@ -264,8 +286,8 @@
         gamma = gamma_new
         multipliers = multipliers + step_size * search
         residual = [residual[n] - step_size * along[n] for n in range(kept)]
-    m_out[...] = multipliers
-    r_out[...] = residual[0]
+    out[0] = multipliers
+    out[1] = residual[0]
 
     for copy in load_copies + part_copies + cpl_copies + d_copies:
         copy.wait_send()
@@ -291,23 +313,28 @@
         f32 = jnp.float32
         vmem = pl.BlockSpec(memory_space=pltpu.VMEM)
         hbm = pl.BlockSpec(memory_space=pl.ANY)
-        tile = jax.ShapeDtypeStruct((rows, width), f32)
         rounds = ITERS + 1
-        m, r = pl.pallas_call(
+        out = pl.pallas_call(
             functools.partial(kernel, nr, nc, near, slots, sc, nrhs),
-            out_shape=(tile, tile),
-            in_specs=[vmem, vmem, vmem, vmem, hbm, hbm],
-            out_specs=(vmem, vmem),
+            out_shape=jax.ShapeDtypeStruct((2, rows, width), f32),
+            in_specs=[hbm] * 6,
+            out_specs=vmem,
             scratch_shapes=[
+                pltpu.VMEM((rows, width), f32),
+                pltpu.VMEM((sc, width), f32),
+                pltpu.VMEM((sc, coarse_inverse.shape[-1]), f32),
+                pltpu.VMEM((sc, width), jnp.int32),
                 pltpu.VMEM((sc, width, width), f32),
                 pltpu.VMEM((len(near), sc, width, width), f32),
+                pltpu.VMEM((sc * width, 2 * width), jnp.bfloat16),
+                pltpu.VMEM((len(near), sc * width, 2 * width), jnp.bfloat16),
                 pltpu.VMEM((len(near), rows, width), f32),
                 pltpu.VMEM((len(near), sc, width), jnp.int32),
                 pltpu.VMEM((len(slots), sc, width), f32),
                 pltpu.VMEM((ndev, rows, lanes), f32),
                 pltpu.VMEM((rounds, len(slots), rows, width), f32),
                 pltpu.VMEM((rounds, ndev, 1, lanes), f32),
-                dma((2,)), dma, dma,
+                dma((6,)), dma, dma,
                 dma((len(slots),)), dma((len(slots),)),
                 dma((len(near),)), dma((len(near),)),
                 dma((len(near),)), dma((len(near),)),
@@ -324,7 +351,7 @@
             local_inverse.reshape(sc, width, width),
             dirichlet.reshape(sc, width, width),
         )
-        return m.reshape(loads.shape), r.reshape(loads.shape)
+        return out[0].reshape(loads.shape), out[1].reshape(loads.shape)
 
     return jax.shard_map(
         body,

time: 36.8 us -> 34.2 us (0.929)
  Pallas kernels: 34 us -> 32.1 us
  local copies, waits for them, and re-layouts: 1.94 us -> 1.28 us
    unnamed x6 -> x0, local copies, waits for them, and re-layouts: 1.94 us -> none
    pallas_call x1, Pallas kernels: 34 us -> 32.1 us  [body(): pl.pallas_call(functools.partial(kernel, nr, nc, near, slots, sc, nrhs),...]
    slice x0 -> x1, local copies, waits for them, and re-layouts: none -> 1.28 us  [body(): return (out[0].reshape(loads.shape), out[1].reshape(loads.shape))]
where the time goes in v2:
time: 34.2 us; the launch traced here: 34 us
  Pallas kernels  32.1 us (94%)
  local copies, waits for them, and re-layouts  1.28 us (4%)
  between operations  0.64 us (2%)
    pallas_call x1, Pallas kernels, body(): pl.pallas_call(functools.partial(kernel, nr, nc, near, slots, sc, nrhs),...  32.1 us
    slice x1, local copies, waits for them, and re-layouts, body(): return (out[0].reshape(loads.shape), out[1].reshape(loads.shape))  1.28 us

profile of v2, /device:TPU:0, one launch (start us, length us, event | category | flops | bytes accessed | tf_op | source)
XLA Modules:
  0.0 34.0 jit_solution(6994946721231553000)
XLA Ops:
  0.6 32.1 %shard_map.77 = f32[2,8,128]{2,1,0:T(8,128)} custom-call(f32[8,128]{1,0:T(8,128)} %bitcast.10, f32[2,128]{1,0:T(2,128)} %bitcast.13, f32[2,16]{1,0:T(2,128)} %bitcast.14, s32[2,128]{1,0:T(2,128)} %bitcast.15, f32[2,128,128]{2,1,0:T(8,128)} %bitcast.8, f32[2,128,128]{2,1,0:T(8,128)} %bitcast.9), custom_call_target="tpu_custom_call" | custom-call | tf_op jit(solution)/shard_map/pallas_call | solution.py:317
  32.8 1.3 %fusion = (f32[1,8,128]{2,1,0:T(8,128)}, f32[1,8,128]{2,1,0:T(8,128)}) fusion(f32[2,8,128]{2,1,0:T(8,128)} %shard_map.77), kind=kLoop, calls=%fused_computation | loop fusion | bytes 16384 | tf_op jit(solution)/shard_map/slice | solution.py:354

commit v3 on v2

--- a/solution.py
+++ b/solution.py
@@ -28,7 +28,7 @@
 
 
 def kernel(nr, nc, near, slots, sc, nrhs, loads_in, cpl_in, cinv_in, part_in, linv, dirich, out,
-           loads, cpl, cinv, part, lbuf, dbuf, lpair, dpair, loads_n, part_n, cpl_n, kt, ub, qb,
+           loads, cpl, cinv, part, lbuf, dbuf, lpair, dpair, loads_n, part_n, cpl_n, kc, kt, ub, qb,
            local_sem, k_send, k_recv, c_send, c_recv, l_send, l_recv, p_send, p_recv, d_send, d_recv,
            u_send, u_recv, q_send, q_recv):
     rows, width = loads.shape
@@ -109,6 +109,8 @@
     for fetch in fetches[:4]:
         fetch.wait()
     tiled = jnp.dot(spread(cinv[...]), tiler, precision=precise, preferred_element_type=jnp.float32)
+    for s in range(sc):
+        kc[0, s : s + 1] = tiled[s * nrhs : s * nrhs + 1]
     kt[0] = jnp.where(of_rhs, tiled, 0.0)
 
     own_position, own_active = index_of(part[...])
@@ -141,7 +143,7 @@
         d_copies.append((src, dst, d_send.at[n], d_recv.at[n], near[n]))
 
     def send_k(k, di, dj):
-        remote(kt.at[0], kt.at[k], k_send, k_recv, (di, dj))
+        remote(kc.at[0], kc.at[k], k_send, k_recv, (di, dj))
 
     others(send_k)
     d_copies = [remote(*args) for args in d_copies]
@@ -246,8 +248,13 @@
         copy.wait_recv()
     lookups = [own_lookup] + [index_of(part_n[n]) for n in range(1, len(near))]
     couplings = [coupling] + [spread(cpl_n[n]) for n in range(1, len(slots))]
-    bytes_k = kt.at[pl.ds(1, ndev - 1)]
+    bytes_k = kc.at[pl.ds(1, ndev - 1)]
     pltpu.make_async_copy(bytes_k, bytes_k, k_recv).wait()
+
+    def widen(k, di, dj):
+        kt[k] = jnp.where(of_rhs, spread(kc[k]), 0.0)
+
+    others(widen)
     fetches[5].wait()
     for copy in d_copies:
         copy.wait_recv()
@@ -331,6 +338,7 @@
                 pltpu.VMEM((len(near), rows, width), f32),
                 pltpu.VMEM((len(near), sc, width), jnp.int32),
                 pltpu.VMEM((len(slots), sc, width), f32),
+                pltpu.VMEM((ndev, sc, lanes), f32),
                 pltpu.VMEM((ndev, rows, lanes), f32),
                 pltpu.VMEM((rounds, len(slots), rows, width), f32),
                 pltpu.VMEM((rounds, ndev, 1, lanes), f32),

time: 34.2 us -> 33.7 us (0.985)
  Pallas kernels: 32.1 us -> 31.6 us
    pallas_call x1, Pallas kernels: 32.1 us -> 31.6 us  [body(): pl.pallas_call(functools.partial(kernel, nr, nc, near, slots, sc, nrhs),...]
where the time goes in v3:
time: 33.7 us; the launch traced here: 33.5 us
  Pallas kernels  31.6 us (94%)
  local copies, waits for them, and re-layouts  1.28 us (4%)
  between operations  0.64 us (2%)
    pallas_call x1, Pallas kernels, body(): pl.pallas_call(functools.partial(kernel, nr, nc, near, slots, sc, nrhs),...  31.6 us
    slice x1, local copies, waits for them, and re-layouts, body(): return (out[0].reshape(loads.shape), out[1].reshape(loads.shape))  1.28 us

profile of v3, /device:TPU:0, one launch (start us, length us, event | category | flops | bytes accessed | tf_op | source)
XLA Modules:
  0.0 33.5 jit_solution(11714001604741653995)
XLA Ops:
  0.6 31.6 %shard_map.77 = f32[2,8,128]{2,1,0:T(8,128)} custom-call(f32[8,128]{1,0:T(8,128)} %bitcast.10, f32[2,128]{1,0:T(2,128)} %bitcast.13, f32[2,16]{1,0:T(2,128)} %bitcast.14, s32[2,128]{1,0:T(2,128)} %bitcast.15, f32[2,128,128]{2,1,0:T(8,128)} %bitcast.8, f32[2,128,128]{2,1,0:T(8,128)} %bitcast.9), custom_call_target="tpu_custom_call" | custom-call | tf_op jit(solution)/shard_map/pallas_call | solution.py:324
  32.2 1.3 %fusion = (f32[1,8,128]{2,1,0:T(8,128)}, f32[1,8,128]{2,1,0:T(8,128)}) fusion(f32[2,8,128]{2,1,0:T(8,128)} %shard_map.77), kind=kLoop, calls=%fused_computation | loop fusion | bytes 16384 | tf_op jit(solution)/shard_map/slice | solution.py:362

commit v4 on v3

--- a/solution.py
+++ b/solution.py
@@ -28,7 +28,7 @@
 
 
 def kernel(nr, nc, near, slots, sc, nrhs, loads_in, cpl_in, cinv_in, part_in, linv, dirich, out,
-           loads, cpl, cinv, part, lbuf, dbuf, lpair, dpair, loads_n, part_n, cpl_n, kc, kt, ub, qb,
+           loads, cpl, cinv, part, lbuf, dbuf, lpair, dpair, loads_n, part_n, cpl_n, dnear, kc, kt, ub, qb,
            local_sem, k_send, k_recv, c_send, c_recv, l_send, l_recv, p_send, p_recv, d_send, d_recv,
            u_send, u_recv, q_send, q_recv):
     rows, width = loads.shape
@@ -43,7 +43,8 @@
 
     def others(step):
         if ndev <= UNROLL:
-            for k in range(1, ndev):
+            far_first = sorted(range(1, ndev), key=lambda k: (-min(k // nc, nr - k // nc), min(k % nc, nc - k % nc) % (nc // 2)))
+            for k in far_first:
                 step(k, k // nc, k % nc)
         else:
             @pl.loop(1, ndev)
@@ -61,7 +62,7 @@
         pltpu.make_async_copy(src, dst, local_sem.at[n])
         for n, (src, dst) in enumerate((
             (cinv_in, cinv), (loads_in, loads), (cpl_in, cpl), (part_in, part),
-            (linv, lbuf), (dirich, dbuf.at[0]),
+            (linv, lbuf), (dirich, dbuf),
         ))
     ]
     for fetch in fetches:
@@ -118,6 +119,8 @@
     own_place = place(0)
     fetches[4].wait()
     split_into(lpair, [lbuf[s] for s in range(sc)])
+    for n in range(1, len(near)):
+        dpair[n] = jnp.zeros(dpair.shape[1:], jnp.bfloat16)
 
     pl.semaphore_wait(barrier, ndev - 1)
 
@@ -132,15 +135,12 @@
     part_copies = [remote(part, part_n.at[n], p_send.at[n], p_recv.at[n], near[n]) for n in range(1, len(near))]
     cpl_copies = [remote(cpl, cpl_n.at[n], c_send.at[n], c_recv.at[n], slots[n]) for n in range(1, len(slots))]
     east_off, west_off = (0, 1 % nc), (0, nc - 1)
+    facing_start = {east_off: 0, west_off: edge, (1 % nr, 0): 2 * edge, (nr - 1, 0): 3 * edge}
     d_copies = []
     for n in range(1, len(near)):
-        if near[n] == east_off:
-            src, dst = dirich.at[pl.ds(0, 1)], dbuf.at[n, pl.ds(0, 1)]
-        elif near[n] == west_off:
-            src, dst = dirich.at[pl.ds(sc - 1, 1)], dbuf.at[n, pl.ds(sc - 1, 1)]
-        else:
-            src, dst = dirich, dbuf.at[n]
-        d_copies.append((src, dst, d_send.at[n], d_recv.at[n], near[n]))
+        subs = {east_off: pl.ds(0, 1), west_off: pl.ds(sc - 1, 1)}.get(near[n], pl.ds(0, sc))
+        src = dirich.at[subs, pl.ds(facing_start[near[n]], edge)]
+        d_copies.append((src, dnear.at[n, subs], d_send.at[n], d_recv.at[n], near[n]))
 
     def send_k(k, di, dj):
         remote(kc.at[0], kc.at[k], k_send, k_recv, (di, dj))
@@ -260,9 +260,19 @@
         copy.wait_recv()
     east, west = near.index(east_off), near.index(west_off)
     upright = [n for n in range(len(near)) if n not in (east, west)]
-    for n in upright:
-        split_into(dpair.at[n], [dbuf[n, s] for s in range(sc)])
-    split_into(dpair.at[east], [dbuf[east, 0], dbuf[west, sc - 1]])
+
+    def edge_into(n, s, pair, at):
+        first = facing_start[near[n]]
+        high, low = split(dnear[n, s].T)
+        pair[at * width : (at + 1) * width, first : first + edge] = high
+        pair[at * width : (at + 1) * width, width + first : width + first + edge] = low
+
+    split_into(dpair.at[0], [dbuf[s] for s in range(sc)])
+    for n in upright[1:]:
+        for s in range(sc):
+            edge_into(n, s, dpair.at[n], s)
+    edge_into(east, 0, dpair.at[east], 0)
+    edge_into(west, sc - 1, dpair.at[east], 1)
     tiles, _, _ = collect(0, count, False)
     residual = [jump_at(tiles, *near[n], lookups[n]) for n in range(len(near))]
 
@@ -332,12 +342,13 @@
                 pltpu.VMEM((sc, coarse_inverse.shape[-1]), f32),
                 pltpu.VMEM((sc, width), jnp.int32),
                 pltpu.VMEM((sc, width, width), f32),
-                pltpu.VMEM((len(near), sc, width, width), f32),
+                pltpu.VMEM((sc, width, width), f32),
                 pltpu.VMEM((sc * width, 2 * width), jnp.bfloat16),
                 pltpu.VMEM((len(near), sc * width, 2 * width), jnp.bfloat16),
                 pltpu.VMEM((len(near), rows, width), f32),
                 pltpu.VMEM((len(near), sc, width), jnp.int32),
                 pltpu.VMEM((len(slots), sc, width), f32),
+                pltpu.VMEM((len(near), sc, width // 4, width), f32),
                 pltpu.VMEM((ndev, sc, lanes), f32),
                 pltpu.VMEM((ndev, rows, lanes), f32),
                 pltpu.VMEM((rounds, len(slots), rows, width), f32),

time: 33.7 us -> 33.3 us (0.988)
  Pallas kernels: 31.6 us -> 31.2 us
    pallas_call x1, Pallas kernels: 31.6 us -> 31.2 us  [body(): pl.pallas_call(functools.partial(kernel, nr, nc, near, slots, sc, nrhs),...]
where the time goes in v4:
time: 33.3 us; the launch traced here: 33.1 us
  Pallas kernels  31.2 us (94%)
  local copies, waits for them, and re-layouts  1.28 us (4%)
  between operations  0.64 us (2%)
    pallas_call x1, Pallas kernels, body(): pl.pallas_call(functools.partial(kernel, nr, nc, near, slots, sc, nrhs),...  31.2 us
    slice x1, local copies, waits for them, and re-layouts, body(): return (out[0].reshape(loads.shape), out[1].reshape(loads.shape))  1.28 us

profile of v4, /device:TPU:0, one launch (start us, length us, event | category | flops | bytes accessed | tf_op | source)
XLA Modules:
  0.0 33.1 jit_solution(12349230082552297372)
XLA Ops:
  0.6 31.2 %shard_map.77 = f32[2,8,128]{2,1,0:T(8,128)} custom-call(f32[8,128]{1,0:T(8,128)} %bitcast.10, f32[2,128]{1,0:T(2,128)} %bitcast.13, f32[2,16]{1,0:T(2,128)} %bitcast.14, s32[2,128]{1,0:T(2,128)} %bitcast.15, f32[2,128,128]{2,1,0:T(8,128)} %bitcast.8, f32[2,128,128]{2,1,0:T(8,128)} %bitcast.9), custom_call_target="tpu_custom_call" | custom-call | tf_op jit(solution)/shard_map/pallas_call | solution.py:334
  31.8 1.3 %fusion = (f32[1,8,128]{2,1,0:T(8,128)}, f32[1,8,128]{2,1,0:T(8,128)}) fusion(f32[2,8,128]{2,1,0:T(8,128)} %shard_map.77), kind=kLoop, calls=%fused_computation | loop fusion | bytes 16384 | tf_op jit(solution)/shard_map/slice | solution.py:373
